TPU v7x, 256 devices: a whole 4x4x8 slice. The times are simulated.
256 devices in a mesh: expert: 32 (over x, y, z_hi), tok: 8 (over z_lo, core).
Axes of the slice: x: 4, y: 4, z: 8 (z_hi: 2, z_lo: 4; z = z_hi * 4 + z_lo), core: 2. Of those that a mesh axis runs over, the one named last changes fastest.
Arguments:
- tokens: bfloat16 [8192, 7168], P(('tok', 'expert')), may hold values from -6 to 6
- w_gate: bfloat16 [64, 7168, 1024], P('expert', None, 'tok'), may hold values from -0.0625 to 0.0625
- w_up: bfloat16 [64, 7168, 1024], P('expert', None, 'tok'), may hold values from -0.0625 to 0.0625
- w_down: bfloat16 [64, 1024, 7168], P('expert', 'tok'), may hold values from -0.1875 to 0.1875
- gates: float32 [8, 64, 32], replicated, may hold values from 0.2 to 1
- dispatch: int32 [8, 64, 32], replicated, may hold values from 0 to 1023, as said below
Outputs:
- combined: bfloat16 [8192, 7168], P(('tok', 'expert'))
Inputs may be any that keep to these rules, and one draw needn't show every extreme that they name: `dispatch`: for each step and expert the 32 indices are different, and at most 2 of them lie in one aligned block of 32 indices (the rows of one device); in every step and for every expert some block holds exactly 2.
All inputs are finite; a program needn't handle non-finite values.
Results may differ from a plain program's by a relative error of at most 0.015.
Values may be sent and summed in bfloat16 or wider, within the bound.
A program may use at most 128 MiB of HBM per device.

v0:
```python
import jax
import jax.numpy as jnp
from jax import lax
from jax.sharding import Mesh
from jax.sharding import PartitionSpec as P

MOST = 2
TOK = ("tok_0", "tok_1")
TOK_EXPERT = ("tok_0", "tok_1", "expert")


def sum_in_order(tiles, axes, turns):
    dims = [lax.axis_size(a) for a in axes]
    tiles = tiles.reshape(*dims, *tiles.shape[1:])
    tiles = tiles.transpose(*turns, *range(len(axes), tiles.ndim))
    tiles = tiles.reshape(-1, *tiles.shape[len(axes) :])
    for k in turns:
        tiles = lax.psum_scatter(tiles, axes[k], scatter_dimension=0, tiled=True)
    return tiles[0]


def cut_along(array, dim, devices):
    before, after = (array.shape[:dim], array.shape[dim + 1 :])
    return jnp.moveaxis(array.reshape(*before, devices, -1, *after), dim, 0)


def scatter_axes(array, axes, turns, dim):
    devices = lax.axis_size(axes)
    return sum_in_order(cut_along(array, dim, devices), axes, turns)


def route_tables(dispatch, rows_dev):
    source = dispatch // rows_dev
    offset = dispatch % rows_dev
    position = jnp.arange(dispatch.shape[-1])
    earlier = (source[..., :, None] == source[..., None, :]) & (
        position[None, :] < position[:, None]
    )
    within = jnp.sum(earlier.astype(jnp.int32), axis=-1)
    return (source, offset, within)


def owner_select(source, offset, within, owner_idx, rows_dev, per_source):
    taken = (
        (source == owner_idx)[..., None] & (within[..., None] == jnp.arange(per_source))
    ).astype(jnp.bfloat16)
    row_table = (offset[..., None] == jnp.arange(rows_dev)).astype(jnp.bfloat16)
    picker = jnp.einsum("ecm,ecr->emr", taken, row_table, preferred_element_type=jnp.float32)
    return picker.astype(jnp.bfloat16).reshape(-1, rows_dev)


def slot_table(source, within, sources, per_source):
    match_source = source[..., None, None] == jnp.arange(sources)[:, None]
    match_within = within[..., None, None] == jnp.arange(per_source)[None, :]
    return (match_source & match_within).astype(jnp.bfloat16)


def expert_partial(chosen, w_gate, w_up, w_down, weight):
    gate_pre = jnp.einsum("...ecd,edh->...ech", chosen, w_gate, preferred_element_type=jnp.float32)
    up_pre = jnp.einsum("...ecd,edh->...ech", chosen, w_up, preferred_element_type=jnp.float32)
    hidden = (jax.nn.silu(gate_pre) * up_pre).astype(jnp.bfloat16)
    down_out = jnp.einsum("...ech,ehd->...ecd", hidden, w_down, preferred_element_type=jnp.float32)
    return (down_out * weight[..., None]).astype(jnp.bfloat16)


def body(tokens, w_gate, w_up, w_down, gates, dispatch):
    sources = lax.axis_size("expert")
    owners = lax.axis_size(TOK)
    rows_dev = tokens.shape[0]
    model_width = tokens.shape[1]
    exp_dev = w_gate.shape[0]
    per_source = MOST
    self_idx = lax.axis_index("expert")
    source, offset, within = route_tables(dispatch, rows_dev)
    mine_source = lax.dynamic_slice_in_dim(source, self_idx * exp_dev, exp_dev, 1)
    mine_within = lax.dynamic_slice_in_dim(within, self_idx * exp_dev, exp_dev, 1)
    gate_mine = lax.dynamic_slice_in_dim(gates, self_idx * exp_dev, exp_dev, 1)
    slots_mine = slot_table(mine_source, mine_within, sources, per_source)
    owner_idx = lax.axis_index(TOK)
    own_source = lax.dynamic_index_in_dim(source, owner_idx, 0, keepdims=False)
    own_offset = lax.dynamic_index_in_dim(offset, owner_idx, 0, keepdims=False)
    own_within = lax.dynamic_index_in_dim(within, owner_idx, 0, keepdims=False)
    picker = owner_select(own_source, own_offset, own_within, self_idx, rows_dev, per_source)
    outgoing = jnp.dot(picker, tokens, preferred_element_type=jnp.float32).astype(jnp.bfloat16)
    outgoing = outgoing.reshape(sources, exp_dev * per_source, model_width)
    arrived = lax.all_to_all(outgoing, "expert", split_axis=0, concat_axis=0, tiled=True)
    everyone = lax.all_gather(arrived[None], TOK, axis=0, tiled=True)
    everyone = everyone.reshape(owners, sources, exp_dev, per_source, model_width)
    chosen = jnp.einsum(
        "secpk,spekd->secd", slots_mine, everyone, preferred_element_type=jnp.float32
    ).astype(jnp.bfloat16)
    partial_value = expert_partial(chosen, w_gate, w_up, w_down, gate_mine)
    summed = scatter_axes(partial_value, TOK, (1, 0), 0).astype(jnp.float32)[0].astype(jnp.bfloat16)
    own_slots = lax.dynamic_index_in_dim(slots_mine, owner_idx, 0, keepdims=False)
    returning = jnp.einsum(
        "ecpk,ecd->pekd", own_slots, summed, preferred_element_type=jnp.float32
    ).astype(jnp.bfloat16)
    returning = returning.reshape(sources, exp_dev * per_source, model_width)
    returned = lax.all_to_all(returning, "expert", split_axis=0, concat_axis=0, tiled=True)
    returned = returned.reshape(sources * exp_dev * per_source, model_width)
    return jnp.dot(picker.T, returned, preferred_element_type=jnp.float32).astype(jnp.bfloat16)


def solution(mesh):
    split = Mesh(mesh.devices.reshape(mesh.shape["expert"], 4, 2), ("expert", "tok_0", "tok_1"))
    in_specs = (
        P(TOK_EXPERT, None),
        P("expert", None, TOK),
        P("expert", None, TOK),
        P("expert", TOK, None),
        P(),
        P(),
    )
    out_specs = P(TOK_EXPERT, None)
    return jax.shard_map(body, mesh=split, in_specs=in_specs, out_specs=out_specs, check_vma=False)
```

profile of v0, /device:TPU:64, one launch (start us, length us, event | category | flops | bytes accessed | tf_op | source)
XLA Modules:
  0.0 428.7 jit_solution(624430313209946607)
XLA Ops:
  6.5 1.0 add_select_fusion
  7.6 1.0 broadcast_compare_fusion
  8.6 1.2 convert_reduce_fusion
  10.0 0.5 convolution_convert_fusion.3
  10.5 1.9 convolution_convert_fusion.1
  12.3 3.1 reshape.65
  15.5 61.8 %all_to_all.10 = bf16[32,4,7168]{2,1,0:T(4,128)(2,1)S(1)} all-to-all(bf16[32,4,7168]{2,1,0:T(4,128)(2,1)S(1)} %reshape.65), channel_id=1, replica_groups=mesh['expert'=32,'tok_0'=4,'tok_1'=2] {'expert'}, dimensions={0} | all-to-all | bytes 3670016 | tf_op jit(solution)/shard_map/all_to_all | solution.py:86
  77.2 1.8 copy.57
  79.0 0.2 reduce-scatter.3.cloned.1.call-start
  79.9 0.1 iota_compare_fusion.2
  80.0 143.8 %all-gather.3.cloned.1.call-done = bf16[256,4,7168]{2,0,1:T(8,128)(2,1)} async-done(((bf16[32,4,7168]{2,0,1:T(8,128)(2,1)}), bf16[256,4,7168]{2,0,1:T(8,128)(2,1)}) %all-gather.3.cloned.1.call-update) | async-done | bytes 14680080 | tf_op jit(solution)/shard_map/all_gather | solution.py:87
  223.8 6.6 %bitcast_convert_fusion = bf16[8,2,32,7168]{3,2,1,0:T(8,128)(2,1)S(1)} fusion(bf16[8,32,2,2,7168]{4,1,0,3,2:T(8,128)(2,1)} %bitcast.74, pred[8,2,32,2]{2,3,1,0:T(4,128)(4,1)S(1)} %iota_compare_fusion.3, pred[8,2,32,32]{3,2,1,0:T(8,128)(4,1)S(1)} %iota_compare_fusion.2), kind=kOutput, calls=%fused_computation.2 | convolution fusion | flops 473464832 | bytes 22037504 | tf_op jit(solution)/shard_map/secpk,spekd->secd/dot_general | solution.py:89
  230.4 3.0 copy-done.2
  233.4 2.1 fusion.12
  235.5 12.2 %fusion = bf16[8,2,32,7168]{3,2,0,1:T(8,128)(2,1)} fusion(f32[8,2,32]{2,0,1:T(8,128)S(1)} %copy.61, bf16[2,128,7168]{2,1,0:T(8,128)(2,1)} %param.9, bf16[2,7168,128]{2,1,0:T(8,128)(2,1)} %param.8, bf16[8,2,32,7168]{3,2,1,0:T(8,128)(2,1)} %copy-done.2, f32[8,2,32,128]{3,2,0,1:T(8,128)S(1)} %fusion.12), kind=kOutput, calls=%fused_computation.1 | convolution fusion | flops 1886781440 | bytes 22284288 | tf_op jit(solution)/shard_map/...ech,ehd->...ecd/dot_general | solution.py:62
  247.7 6.7 %copy.62 = bf16[2,4,1,2,32,7168]{5,4,3,1,0,2:T(8,128)(2,1)} copy(bf16[2,4,1,2,32,7168]{5,4,0,1,3,2:T(8,128)(2,1)} %bitcast.73) | data formatting | bytes 14680064 | tf_op jit(solution)/shard_map/transpose | solution.py:15
  254.5 23.0 %reduce-scatter.3.cloned.1.call-done = bf16[4,1,2,32,7168]{4,3,2,1,0:T(8,128)(2,1)} async-done(((bf16[8,1,2,32,7168]{4,3,2,1,0:T(8,128)(2,1)}), bf16[4,1,2,32,7168]{4,3,2,1,0:T(8,128)(2,1)}) %reduce-scatter.3.cloned.1.call-update) | async-done | bytes 3670032 | tf_op jit(solution)/shard_map/reduce_scatter | solution.py:18
  277.5 0.2 broadcast_and_fusion
  277.7 77.6 %reduce-scatter.5.cloned.1.call-done = bf16[1,1,2,32,7168]{4,3,2,1,0:T(8,128)(2,1)} async-done(((bf16[4,1,2,32,7168]{4,3,2,1,0:T(8,128)(2,1)}), bf16[1,1,2,32,7168]{4,3,2,1,0:T(8,128)(2,1)}) %reduce-scatter.5.cloned.1.call-update) | async-done | bytes 917520 | tf_op jit(solution)/shard_map/reduce_scatter | solution.py:18
  355.3 1.8 convolution_convert_fusion
  357.2 1.4 copy.64
  358.6 59.4 %all_to_all.11 = bf16[32,4,7168]{2,1,0:T(4,128)(2,1)} all-to-all(bf16[32,4,7168]{2,1,0:T(4,128)(2,1)S(1)} %copy.64), channel_id=1, replica_groups=mesh['expert'=32,'tok_0'=4,'tok_1'=2] {'expert'}, dimensions={0} | all-to-all | bytes 3670016 | tf_op jit(solution)/shard_map/all_to_all | solution.py:99
  418.0 2.9 reshape.69
  421.0 1.2 convolution_convert_fusion.2
  (26 shorter events, 1.0 us)
Async XLA Ops:
  6.5 3.9 copy-start
  6.5 217.3 %all-gather.3.cloned.1.call-start = ((), (), s32[]{:S(2)}) async-start(), calls=%async_computation.6 | async-start | bytes 16515072 | tf_op jit(solution)/shard_map/all_gather | solution.py:87
  77.2 2.4 copy-start.3
  79.0 198.5 %reduce-scatter.3.cloned.1.call-start = ((), (), s32[]{:S(2)}) async-start(), calls=%async_computation.4 | async-start | bytes 11010048 | tf_op jit(solution)/shard_map/reduce_scatter | solution.py:18
  223.8 9.6 %copy-start.4 = (bf16[2,7168,128]{2,1,0:T(8,128)(2,1)S(1)}, bf16[2,7168,128]{2,1,0:T(8,128)(2,1)}, u32[]{:S(2)}) copy-start(bf16[2,7168,128]{2,1,0:T(8,128)(2,1)} %param.7) | copy-start | bytes 11010052
  230.4 3.0 copy-start.2
  254.4 100.9 %reduce-scatter.5.cloned.1.call-start = ((), (), s32[]{:S(2)}) async-start(), calls=%async_computation.5 | async-start | bytes 4587520 | tf_op jit(solution)/shard_map/reduce_scatter | solution.py:18
  358.6 63.5 %copy-start.1 = (bf16[32,7168]{1,0:T(8,128)(2,1)S(1)}, bf16[32,7168]{1,0:T(8,128)(2,1)}, u32[]{:S(2)}) copy-start(bf16[32,7168]{1,0:T(8,128)(2,1)} %param.6) | copy-start | bytes 1376260
Sparse Core Ops, SparseCore 0:
  79.2 144.5 all-gather.2
  254.6 22.8 reduce-scatter.2
  280.1 75.2 reduce-scatter.4
where the time goes:
time: 429 us
  waiting for transfers between devices  244 us (57%)
  blocking collectives  121 us (28%)
  matrix products  26.2 us (6%)
  local copies, waits for them, and re-layouts  19.8 us (5%)
  between operations  13.3 us (3%)
    all_gather x1, waiting for transfers between devices, body(): everyone = lax.all_gather(arrived[None], TOK, axis=0, tiled=True)  144 us
    reduce_scatter x2, waiting for transfers between devices, sum_in_order(): tiles = lax.psum_scatter(tiles, axes[k], scatter_dimension=0, tiled=True)  101 us
    all_to_all x1, blocking collectives, body(): lax.all_to_all(outgoing, 'expert', split_axis=0, concat_axis=0, tiled=True)  61.8 us
    all_to_all x1, blocking collectives, body(): lax.all_to_all(returning, 'expert', split_axis=0, concat_axis=0, tiled=True)  59.4 us
    dot_general x1, matrix products, expert_partial(): jnp.einsum('...ech,ehd->...ecd', hidden, w_down, preferred_element_type=j...  12.2 us
  transfers between devices with their start and end apart: 3, of which 3 were waited for; matrix products, arithmetic and copies ran while one was open for 0% of the time, Pallas kernels for 0%

commit v1 on v0

v1 whole, which is shorter than its diff:
```python
import jax
import jax.numpy as jnp
from jax import lax
from jax.experimental import pallas as pl
from jax.experimental.pallas import tpu as pltpu
from jax.sharding import Mesh
from jax.sharding import PartitionSpec as P

NX, NY, NH, NL, NC = 4, 4, 2, 4, 2
NZ = NH * NL
COLS = NX * NY
D1 = 4096
SLOTS = 4
BF = jnp.bfloat16
F32 = jnp.float32
ANY = pl.BlockSpec(memory_space=pl.ANY)
VMEM = pl.BlockSpec(memory_space=pltpu.VMEM)
DMA = pltpu.SemaphoreType.DMA


def z_of(z):
    z = lax.rem(z + NZ, NZ)
    return {"zh": lax.div(z, NL), "zl": lax.rem(z, NL)}


def remote(src, dst, send, recv, device):
    return pltpu.make_async_remote_copy(
        src_ref=src, dst_ref=dst, send_sem=send, recv_sem=recv,
        device_id=device, device_id_type=pl.DeviceIdType.MESH)


def greet(devices):
    barrier = pltpu.get_barrier_semaphore()
    for device in devices:
        pl.semaphore_signal(barrier, inc=1, device_id=device, device_id_type=pl.DeviceIdType.MESH)
    pl.semaphore_wait(barrier, len(devices))


def xy_targets():
    x, y = lax.axis_index("x"), lax.axis_index("y")
    found = []
    for d in range(1, COLS):
        found.append((lax.rem(x + d // NY, NX), lax.rem(y + d % NY, NY)))
    return found


def xy_devices():
    return [{"x": tx, "y": ty} for tx, ty in xy_targets()]


def xy_copies(src, dst, send, recv):
    me = lax.axis_index("x") * NY + lax.axis_index("y")
    return [
        remote(src.at[tx * NY + ty], dst.at[me], send.at[d], recv.at[d], {"x": tx, "y": ty})
        for d, (tx, ty) in enumerate(xy_targets())
    ]


def my_z():
    return lax.axis_index("zh") * NL + lax.axis_index("zl")


def pair_kernel(own_ref, out_ref, relay, send, recv):
    z = my_z()
    rows, width = out_ref.shape
    half = rows // 2
    greet([z_of(z + 2), z_of(z - 2)])
    first = []
    for d, step in enumerate((2, -2)):
        part = pl.ds(d * half, half)
        copy = remote(own_ref.at[part, pl.ds(0, width)], relay.at[d], send.at[d], recv.at[d], z_of(z + step))
        copy.start()
        first.append(copy)
    second = []
    for d, step in enumerate((2, -2)):
        part = pl.ds(d * half, half)
        first[d].wait_recv()
        copy = remote(relay.at[d], out_ref.at[part], send.at[2 + d], recv.at[2 + d], z_of(z + step))
        copy.start()
        second.append(copy)
    for copy in first:
        copy.wait_send()
    for copy in second:
        copy.wait()


def pair_exchange(own, width, cid):
    rows = own.shape[0]
    return pl.pallas_call(
        pair_kernel,
        out_shape=jax.ShapeDtypeStruct((rows, width), BF),
        in_specs=[ANY], out_specs=ANY,
        scratch_shapes=[pltpu.VMEM((2, rows // 2, width), BF), DMA((4,)), DMA((4,))],
        compiler_params=pltpu.CompilerParams(collective_id=cid, has_side_effects=True),
        name="pair_exchange",
    )(own)


def ring_kernel(tok_ref, blk_ref, all_ref, got_ref, xs, xr, us, ur, ds, dr, ls):
    z = my_z()
    rows = tok_ref.shape[0]
    half = rows // 2
    width = all_ref.shape[2]
    start_col = tok_ref.shape[1] - width
    greet(xy_devices() + [z_of(z + 1), z_of(z - 1)])
    me = lax.axis_index("x") * NY + lax.axis_index("y")

    def hop(t, h, up):
        who = lax.rem(z + (-(t - 1) if up else t - 1) + NZ, NZ)
        part = pl.ds(h * half, half)
        if t == 1:
            src = tok_ref.at[part, pl.ds(start_col, width)]
        else:
            src = all_ref.at[who, part]
        send, recv = (us, ur) if up else (ds, dr)
        return remote(src, all_ref.at[who, part], send.at[t - 1, h], recv.at[t - 1, h], z_of(z + (1 if up else -1)))

    last = NZ // 2
    hops = [(t, h, up) for t in range(1, last + 1) for h in range(2) for up in (True, False)
            if t < last or (h == 0) == up]
    for t, h, up in hops:
        if t == 1:
            hop(t, h, up).start()
    blocks = xy_copies(blk_ref, got_ref, xs, xr)
    for copy in blocks:
        copy.start()
    own = [pltpu.make_async_copy(tok_ref.at[:, pl.ds(start_col, width)], all_ref.at[z], ls.at[0]),
           pltpu.make_async_copy(blk_ref.at[me], got_ref.at[me], ls.at[1])]
    for copy in own:
        copy.start()
    for t, h, up in hops:
        hop(t, h, up).wait_recv()
        if (t + 1, h, up) in hops:
            hop(t + 1, h, up).start()
    for t, h, up in hops:
        hop(t, h, up).wait_send()
    for copy in blocks:
        copy.wait()
    for copy in own:
        copy.wait()


def ring_and_plane(tokens, blocks, cid):
    rows = tokens.shape[0]
    width = tokens.shape[1] - D1
    return pl.pallas_call(
        ring_kernel,
        out_shape=(jax.ShapeDtypeStruct((NZ, rows, width), BF), jax.ShapeDtypeStruct(blocks.shape, BF)),
        in_specs=[ANY, ANY], out_specs=(ANY, ANY),
        scratch_shapes=[DMA((COLS - 1,)), DMA((COLS - 1,))] + [DMA((NZ // 2, 2))] * 4 + [DMA((2,))],
        compiler_params=pltpu.CompilerParams(collective_id=cid, has_side_effects=True),
        name="ring_and_plane",
    )(tokens, blocks)


def line_kernel(row_ref, blk_ref, wg_ref, wu_ref, wd_ref, all_ref, got_ref, og_ref, ou_ref, od_ref,
                xs, xr, us, ur, ds, dr, ws, wr, ls):
    zl = lax.axis_index("zl")
    experts = row_ref.shape[0]
    me = lax.axis_index("x") * NY + lax.axis_index("y")
    above, below = lax.rem(zl + 1, NL), lax.rem(zl + NL - 1, NL)
    other = {"c": 1 - lax.axis_index("c")}
    greet(xy_devices() + [{"zl": above}, {"zl": below}, other])

    def hop(i, e, up):
        who = lax.rem(zl + (-i if up else i) + NL, NL)
        src = row_ref.at[e] if i == 0 else all_ref.at[e, who]
        send, recv = (us, ur) if up else (ds, dr)
        return remote(src, all_ref.at[e, who], send.at[i, e], recv.at[i, e], {"zl": above if up else below})

    def sends(i, up):
        return (zl < NL - 1) & (zl >= i) if up else (zl > 0) & (zl + i < NL)

    def gets(i, up):
        return zl - 1 - i >= 0 if up else zl + 1 + i < NL

    for e in range(experts):
        for up in (True, False):
            @pl.when(sends(0, up))
            def _():
                hop(0, e, up).start()
    blocks = xy_copies(blk_ref, got_ref, xs, xr)
    for copy in blocks:
        copy.start()
    weights = [remote(a, b, ws.at[i], wr.at[i], other)
               for i, (a, b) in enumerate(((wg_ref, og_ref), (wu_ref, ou_ref), (wd_ref, od_ref)))]
    for copy in weights:
        copy.start()
    own = [pltpu.make_async_copy(row_ref.at[e], all_ref.at[e, zl], ls.at[e]) for e in range(experts)]
    own.append(pltpu.make_async_copy(blk_ref.at[me], got_ref.at[me], ls.at[experts]))
    for copy in own:
        copy.start()
    for i in range(NL - 1):
        for e in range(experts):
            for up in (True, False):
                @pl.when(gets(i, up))
                def _():
                    hop(i, e, up).wait_recv()
                if i < NL - 2:
                    @pl.when(sends(i + 1, up))
                    def _():
                        hop(i + 1, e, up).start()
    for i in range(NL - 1):
        for e in range(experts):
            for up in (True, False):
                @pl.when(sends(i, up))
                def _():
                    hop(i, e, up).wait_send()
    for copy in blocks + weights:
        copy.wait()
    for copy in own:
        copy.wait()


def line_and_plane(rows, blocks, w_gate, w_up, w_down, cid):
    experts, cap, width = rows.shape
    shapes = [(experts, NL, cap, width), blocks.shape, w_gate.shape, w_up.shape, w_down.shape]
    return pl.pallas_call(
        line_kernel,
        out_shape=tuple(jax.ShapeDtypeStruct(s, BF) for s in shapes),
        in_specs=[ANY] * 5, out_specs=(ANY,) * 5,
        scratch_shapes=[DMA((COLS - 1,)), DMA((COLS - 1,))] + [DMA((NL - 1, experts))] * 4
        + [DMA((3,)), DMA((3,)), DMA((experts + 1,))],
        compiler_params=pltpu.CompilerParams(collective_id=cid, has_side_effects=True),
        name="line_and_plane",
    )(rows, blocks, w_gate, w_up, w_down)


def add_into(dst, a, b, width, extra=None, chunk=512):
    @pl.loop(0, width // chunk)
    def _(i):
        part = pl.ds(pl.multiple_of(i * chunk, chunk), chunk)
        total = a[:, part].astype(F32) + b[:, part].astype(F32)
        if extra is not None:
            total = total + extra[:, part].astype(F32)
        dst[:, part] = total.astype(BF)


def line_sum_kernel(part_ref, blk_ref, out_ref, got_ref, ub, db, xs, xr, us, ur, ds, dr, ls):
    zl = lax.axis_index("zl")
    experts = part_ref.shape[0]
    width = part_ref.shape[3]
    me = lax.axis_index("x") * NY + lax.axis_index("y")
    above, below = lax.rem(zl + 1, NL), lax.rem(zl + NL - 1, NL)
    greet(xy_devices() + [{"zl": above}, {"zl": below}])

    def hop(j, e, up, fresh):
        buf = ub if up else db
        slot = j - 1 if up else j
        send, recv = (us, ur) if up else (ds, dr)
        src = part_ref.at[e, j] if fresh else buf.at[slot, e]
        return remote(src, buf.at[slot, e], send.at[slot, e], recv.at[slot, e], {"zl": above if up else below})

    order = [(NL - 1 - i, i) for i in range(NL - 1)]
    for ju, jd in order:
        for e in range(experts):
            @pl.when(zl == 0)
            def _():
                hop(ju, e, True, True).start()

            @pl.when(zl == NL - 1)
            def _():
                hop(jd, e, False, True).start()
    blocks = xy_copies(blk_ref, got_ref, xs, xr)
    for copy in blocks:
        copy.start()
    own = pltpu.make_async_copy(blk_ref.at[me], got_ref.at[me], ls)
    own.start()
    for ju, jd in order:
        for e in range(experts):
            for up, j in ((True, ju), (False, jd)):
                inner = (zl > 0) & (zl <= j) if up else (zl < NL - 1) & (zl >= j)
                passes = (zl > 0) & (zl < j) if up else (zl < NL - 1) & (zl > j)
                slot = j - 1 if up else j
                buf = ub if up else db

                @pl.when(inner)
                def _():
                    hop(j, e, up, False).wait_recv()

                @pl.when(passes)
                def _():
                    add_into(buf.at[slot, e], buf.at[slot, e], part_ref.at[e, j], width)
                    hop(j, e, up, False).start()
    for e in range(experts):
        @pl.when(zl == 0)
        def _():
            add_into(out_ref.at[e], part_ref.at[e, 0], db.at[0, e], width)

        @pl.when(zl == NL - 1)
        def _():
            add_into(out_ref.at[e], part_ref.at[e, NL - 1], ub.at[NL - 2, e], width)
        for mid in range(1, NL - 1):
            @pl.when(zl == mid)
            def _():
                add_into(out_ref.at[e], part_ref.at[e, mid], ub.at[mid - 1, e], width, db.at[mid, e])
    for ju, jd in order:
        for e in range(experts):
            @pl.when(zl < ju)
            def _():
                hop(ju, e, True, False).wait_send()

            @pl.when(zl > jd)
            def _():
                hop(jd, e, False, False).wait_send()
    for copy in blocks:
        copy.wait()
    own.wait()


def line_sum_and_plane(parts, blocks, cid):
    experts, _, cap, width = parts.shape
    buf = pltpu.VMEM((NL - 1, experts, cap, width), BF)
    return pl.pallas_call(
        line_sum_kernel,
        out_shape=(jax.ShapeDtypeStruct((experts, cap, width), BF), jax.ShapeDtypeStruct(blocks.shape, BF)),
        in_specs=[VMEM, ANY], out_specs=(VMEM, ANY),
        scratch_shapes=[buf, buf, DMA((COLS - 1,)), DMA((COLS - 1,))] + [DMA((NL - 1, experts))] * 4 + [DMA],
        compiler_params=pltpu.CompilerParams(collective_id=cid, has_side_effects=True),
        name="line_sum_and_plane",
    )(parts, blocks)


def ring_sum_kernel(part_ref, blk_ref, out_ref, got_ref, ub, db, xs, xr, us, ur, ds, dr, ls):
    z = my_z()
    rows, width = out_ref.shape
    half = rows // 2
    me = lax.axis_index("x") * NY + lax.axis_index("y")
    greet(xy_devices() + [z_of(z + 1), z_of(z - 1)])
    last = NZ // 2

    def spot(t, up):
        return lax.rem(z + (last - t if up else t - last) + NZ, NZ)

    def rows_of(h):
        return pl.ds(h * half, half)

    def hop(t, h, up, fresh):
        buf = ub if up else db
        send, recv = (us, ur) if up else (ds, dr)
        src = part_ref.at[spot(t, up), rows_of(h)] if fresh else buf.at[t - 1, h]
        return remote(src, buf.at[t, h], send.at[t, h], recv.at[t, h], z_of(z + (1 if up else -1)))

    def fresh_of(t, h, up):
        return t == 0 or (t == 1 and (h == 0) != up)

    hops = [(t, h, up) for t in range(last) for h in range(2) for up in (True, False)
            if t > 0 or (h == 0) == up]
    for t, h, up in hops:
        if fresh_of(t, h, up):
            hop(t, h, up, True).start()
    blocks = xy_copies(blk_ref, got_ref, xs, xr)
    for copy in blocks:
        copy.start()
    own = pltpu.make_async_copy(blk_ref.at[me], got_ref.at[me], ls)
    own.start()
    for t, h, up in hops:
        buf = ub if up else db
        hop(t, h, up, fresh_of(t, h, up)).wait_recv()
        if t < last - 1:
            add_into(buf.at[t, h], buf.at[t, h], part_ref.at[spot(t + 1, up), rows_of(h)], width)
            hop(t + 1, h, up, False).start()
    for h in range(2):
        add_into(out_ref.at[rows_of(h)], part_ref.at[z, rows_of(h)], ub.at[last - 1, h], width, db.at[last - 1, h])
    for t, h, up in hops:
        hop(t, h, up, fresh_of(t, h, up)).wait_send()
    for copy in blocks:
        copy.wait()
    own.wait()


def ring_sum_and_plane(parts, blocks, cid):
    _, rows, width = parts.shape
    buf = pltpu.VMEM((NZ // 2, 2, rows // 2, width), BF)
    return pl.pallas_call(
        ring_sum_kernel,
        out_shape=(jax.ShapeDtypeStruct((rows, width), BF), jax.ShapeDtypeStruct(blocks.shape, BF)),
        in_specs=[VMEM, ANY], out_specs=(VMEM, ANY),
        scratch_shapes=[buf, buf, DMA((COLS - 1,)), DMA((COLS - 1,))] + [DMA((NZ // 2, 2))] * 4 + [DMA],
        compiler_params=pltpu.CompilerParams(collective_id=cid, has_side_effects=True),
        name="ring_sum_and_plane",
    )(parts, blocks)


def mm(a, b, dtype=BF):
    return jnp.dot(a, b, preferred_element_type=F32).astype(dtype)


def body(tokens, w_gate, w_up, w_down, gates, dispatch):
    rows, width = tokens.shape
    experts = w_gate.shape[0]
    cap = dispatch.shape[-1]
    x, y, zh = lax.axis_index("x"), lax.axis_index("y"), lax.axis_index("zh")
    zl, c = lax.axis_index("zl"), lax.axis_index("c")
    col = x * NY + y
    span = NH * rows

    def of_parity(a):
        a = a.reshape(NL, NC, COLS, NH, experts, cap)
        a = lax.dynamic_index_in_dim(a, c, 1, keepdims=False)
        return lax.dynamic_index_in_dim(a, zh, 2, keepdims=False)

    picks = of_parity(dispatch)
    block = picks // span
    earlier = (block[..., :, None] == block[..., None, :]) & (jnp.arange(cap)[None, :] < jnp.arange(cap)[:, None])
    place = jnp.sum(earlier.astype(jnp.int32), axis=-1)

    here = jnp.where(block == col, (picks % span) * SLOTS + place, -1)
    table = here[..., None, None, :] == (jnp.arange(span)[None, :] * SLOTS + jnp.arange(SLOTS)[:, None])[..., None]
    table = jnp.any(table, axis=-1)
    pick1 = lax.dynamic_index_in_dim(table, zl, 0, keepdims=False)
    pick1 = pick1.reshape(COLS * experts * SLOTS, NH, rows).astype(BF)
    pick2 = table.transpose(1, 0, 2, 3, 4).reshape(COLS, NL, experts, SLOTS, NH, 1, rows)
    pick2 = pick2 & (jnp.arange(NL)[:, None, None, None, None, None] == jnp.arange(NL)[:, None])
    pick2 = pick2.reshape(COLS * NL * experts * SLOTS, NZ * rows).astype(BF)

    mine = lax.dynamic_index_in_dim(block * SLOTS + place, col, 1, keepdims=False)
    mine = mine.transpose(1, 0, 2)
    fit = mine[..., None] == jnp.arange(COLS * SLOTS)
    fit = fit.reshape(experts, NL, cap, COLS, SLOTS)
    fit1 = lax.dynamic_index_in_dim(fit, zl, 1, keepdims=False)
    same_e = jnp.eye(experts, dtype=bool)
    fit1 = fit1[:, :, :, None, :] & same_e[:, None, None, :, None]
    fit1 = fit1.reshape(experts * cap, COLS * experts * SLOTS).astype(BF)
    same_k = jnp.eye(NL, dtype=bool)
    fit2 = fit[:, :, :, :, None, None, :] & same_k[None, :, None, None, :, None, None] & same_e[:, None, None, None, None, :, None]
    fit2 = fit2.reshape(experts * NL * cap, COLS * NL * experts * SLOTS).astype(BF)
    weight = lax.dynamic_index_in_dim(of_parity(gates), col, 1, keepdims=False)
    weight = weight.transpose(1, 0, 2).reshape(experts, NL * cap, 1)

    other = pair_exchange(tokens, D1, 1)
    pick_own = lax.dynamic_index_in_dim(pick1, zh, 1, keepdims=False)
    pick_other = lax.dynamic_index_in_dim(pick1, 1 - zh, 1, keepdims=False)
    out1 = (mm(pick_own, tokens[:, :D1], F32) + mm(pick_other, other, F32)).astype(BF)
    everyone, got1 = ring_and_plane(tokens, out1.reshape(COLS, experts * SLOTS, D1), 2)
    rows1 = mm(fit1, got1.reshape(-1, D1)).reshape(experts, cap, D1)
    out2 = mm(pick2, everyone.reshape(NZ * rows, width - D1))
    lines, got2, og, ou, od = line_and_plane(
        rows1, out2.reshape(COLS, NL * experts * SLOTS, width - D1), w_gate, w_up, w_down, 3)
    x1 = lines.reshape(experts, NL * cap, D1)
    x2 = mm(fit2, got2.reshape(-1, width - D1)).reshape(experts, NL * cap, width - D1)
    chosen = jnp.concatenate([x1, x2], axis=2)

    def einsum(a, b):
        return jnp.einsum("eck,ekn->ecn", a, b, preferred_element_type=F32)

    down = 0.0
    for g, u, d in ((w_gate, w_up, w_down), (og, ou, od)):
        hidden = (jax.nn.silu(einsum(chosen, g)) * einsum(chosen, u)).astype(BF)
        down = down + einsum(hidden, d)
    partial = (down * weight).astype(BF)
    back1 = partial[:, :, :D1].reshape(experts, NL, cap, D1)
    back2 = mm(fit2.T, partial[:, :, D1:].reshape(experts * NL * cap, width - D1))
    summed, home2 = line_sum_and_plane(back1, back2.reshape(COLS, NL * experts * SLOTS, width - D1), 4)
    give1 = mm(fit1.T, summed.reshape(experts * cap, D1))
    sums2 = mm(pick2.T, home2.reshape(-1, width - D1)).reshape(NZ, rows, width - D1)
    final2, home1 = ring_sum_and_plane(sums2, give1.reshape(COLS, experts * SLOTS, D1), 5)
    home1 = home1.reshape(-1, D1)
    returned = pair_exchange(mm(pick_other.T, home1), D1, 6)
    final1 = (mm(pick_own.T, home1, F32) + returned.astype(F32)).astype(BF)
    return jnp.concatenate([final1, final2], axis=1)


def solution(mesh):
    split = Mesh(mesh.devices.reshape(NX, NY, NH, NL, NC), ("x", "y", "zh", "zl", "c"))
    expert, tok = ("x", "y", "zh"), ("zl", "c")
    in_specs = (P(tok + expert, None), P(expert, None, tok), P(expert, None, tok), P(expert, tok, None), P(), P())
    return jax.shard_map(body, mesh=split, in_specs=in_specs, out_specs=P(tok + expert, None), check_vma=False)
```

time: 429 us -> 271 us (0.63)
  waiting for transfers between devices: 244 us -> 0 us
  Pallas kernels: 0 us -> 203 us
  blocking collectives: 121 us -> 0 us
  matrix products: 26.2 us -> 47.6 us
  between operations: 13.3 us -> 0.35 us
  local copies, waits for them, and re-layouts: 19.8 us -> 7.99 us
  other arithmetic: 3.54 us -> 9.43 us
    pallas_call x0 -> x6, Pallas kernels: none -> 203 us  [the longest x1 66 us: line_sum_and_plane(): pl.pallas_call(line_sum_kernel, out_shape=(jax.ShapeDtypeStruct((experts,...]
    all_gather x1 -> x0, waiting for transfers between devices: 144 us -> none  [body(): everyone = lax.all_gather(arrived[None], TOK, axis=0, tiled=True)]
    all_to_all x2 -> x0, blocking collectives: 121 us -> none  [the longest x1 61.8 us: body(): lax.all_to_all(outgoing, 'expert', split_axis=0, concat_axis=0, tiled=True)]
    reduce_scatter x2 -> x0, waiting for transfers between devices: 101 us -> none  [sum_in_order(): tiles = lax.psum_scatter(tiles, axes[k], scatter_dimension=0, tiled=True)]
    dot_general x7 -> x14, matrix products: 26.2 us -> 47.6 us  [the longest x10 24.4 us: mm(): return jnp.dot(a, b, preferred_element_type=F32).astype(dtype)]
    reshape x3 -> x1, local copies, waits for them, and re-layouts: 7.48 us -> 0.1 us  [body(): pick1 = pick1.reshape(COLS * experts * SLOTS, NH, rows).astype(BF)]
    transpose x1 -> x3, local copies, waits for them, and re-layouts: 6.73 us -> 0.02 us  [the longest x2 0.02 us: body(): weight = weight.transpose(1, 0, 2).reshape(experts, NL * cap, 1)]
  transfers between devices with their start and end apart: 3 -> 0, of which waited for: 3 -> 0; matrix products, arithmetic and copies ran while one was open for 0% -> 0% of each run, Pallas kernels for 0% -> 0%
where the time goes in v1:
time: 271 us; the launch traced here: 268 us
  Pallas kernels  203 us (75%)
  matrix products  47.6 us (18%)
  other arithmetic  9.43 us (3%)
  local copies, waits for them, and re-layouts  7.99 us (3%)
    pallas_call x1, Pallas kernels, line_sum_and_plane(): pl.pallas_call(line_sum_kernel, out_shape=(jax.ShapeDtypeStruct((experts,...  66 us
    pallas_call x1, Pallas kernels, line_and_plane(): pl.pallas_call(line_kernel, out_shape=tuple((jax.ShapeDtypeStruct(s, BF)...  45 us
    pallas_call x2, Pallas kernels, pair_exchange(): pl.pallas_call(pair_kernel, out_shape=jax.ShapeDtypeStruct((rows, width),...  32.4 us
    pallas_call x1, Pallas kernels, ring_sum_and_plane(): pl.pallas_call(ring_sum_kernel, out_shape=(jax.ShapeDtypeStruct((rows, wi...  30.8 us
    pallas_call x1, Pallas kernels, ring_and_plane(): pl.pallas_call(ring_kernel, out_shape=(jax.ShapeDtypeStruct((NZ, rows, wi...  28.5 us
    dot_general x10, matrix products, mm(): return jnp.dot(a, b, preferred_element_type=F32).astype(dtype)  24.4 us
    dot_general x4, matrix products, einsum(): return jnp.einsum('eck,ekn->ecn', a, b, preferred_element_type=F32)  23.2 us

profile of v1, /device:TPU:64, one launch (start us, length us, event | category | flops | bytes accessed | tf_op | source)
XLA Modules:
  0.0 268.2 jit_solution(15179226852200706765)
XLA Ops:
  0.2 1.0 copy.59
  2.6 3.0 %convert_reduce_fusion = s32[4,16,2,32]{3,2,1,0:T(2,128)S(1)} fusion(s32[4,16,2,32]{3,2,1,0:T(2,128)S(1)} %and_select_fusion.1, pred[32,32]{1,0:T(8,128)(4,1)S(1)} %iota_compare_fusion), kind=kLoop, calls=%fused_computation.18 | loop fusion | flops 520192 | bytes 33792 | tf_op jit(solution)/shard_map/reduce_sum | solution.py:406
  5.8 2.0 compare_reduce_fusion
  12.6 18.8 %pair_exchange.2 = bf16[32,4096]{1,0:T(8,128)(2,1)} custom-call(bf16[32,7168]{1,0:T(8,128)(2,1)} %tok_ref.1), custom_call_target="tpu_custom_call" | custom-call | tf_op jit(solution)/shard_map/pair_exchange/pallas_call | solution.py:89
  31.9 2.4 fusion.4.blk_ref
  34.3 28.5 %ring_and_plane.1 = (bf16[8,32,3072]{2,1,0:T(8,128)(2,1)}, bf16[16,8,4096]{2,1,0:T(8,128)(2,1)}) custom-call(bf16[32,7168]{1,0:T(8,128)(2,1)} %tok_ref.1, bf16[16,8,4096]{2,1,0:T(8,128)(2,1)} %fusion.4.blk_ref), custom_call_target="tpu_custom_call" | custom-call | tf_op jit(solution)/shard_map/ring_and_plane/pallas_call | solution.py:146
  62.8 2.4 convolution_convert_fusion.1
  65.2 4.1 %convolution_convert_fusion.4 = bf16[512,3072]{1,0:T(8,128)(2,1)} fusion(pred[512,256]{1,0:T(32,128)(4,1)S(1)} %and.165, bf16[256,3072]{1,0:T(8,128)(2,1)} %bitcast.90), kind=kOutput, calls=%fused_computation.14 | convolution fusion | flops 806879232 | bytes 4849664 | tf_op jit(solution)/shard_map/dot_general | solution.py:386
  69.3 45.0 %line_and_plane.1 = (bf16[2,4,32,4096]{3,2,1,0:T(8,128)(2,1)}, bf16[16,32,3072]{2,1,0:T(8,128)(2,1)}, bf16[2,7168,128]{2,1,0:T(8,128)(2,1)}, bf16[2,7168,128]{2,1,0:T(8,128)(2,1)}, bf16[2,128,7168]{2,1,0:T(8,128)(2,1)}) custom-call(bf16[2,32,4096]{2,1,0:T(8,128)(2,1)} %bitcast.89, bf16[16,32,3072]{2,1,0:T(8,128)(2,1)} %bitcast.74, ...), custom_call_target="tpu_custom_call" | custom-call | tf_op jit(solution)/shard_map/line_and_plane/pallas_call | solution.py:218
  114.3 3.1 %convolution_convert_fusion.6 = bf16[256,3072]{1,0:T(8,128)(2,1)S(1)} fusion(pred[256,512]{0,1:T(32,128)(4,1)S(1)} %and.177, bf16[512,3072]{1,0:T(8,128)(2,1)} %bitcast.87), kind=kOutput, calls=%fused_computation.16 | convolution fusion | flops 806092800 | bytes 4849664 | tf_op jit(solution)/shard_map/dot_general | solution.py:386
  117.4 3.3 %fusion.35 = f32[2,128,128]{2,1,0:T(8,128)S(1)} fusion(bf16[2,7168,128]{2,1,0:T(8,128)(2,1)} %get-tuple-element.20, bf16[2,128,3072]{2,1,0:T(8,128)(2,1)S(1)} %bitcast.77, bf16[2,128,4096]{2,1,0:T(8,128)(2,1)S(1)} %bitcast.83), kind=kOutput, calls=%fused_computation.79 | convolution fusion | flops 477102080 | bytes 7471104 | tf_op jit(solution)/shard_map/eck,ekn->ecn/dot_general | solution.py:445
  120.8 1.1 fusion.36
  121.9 9.0 %fusion.8 = f32[2,128,7168]{2,1,0:T(8,128)} fusion(bf16[2,128,7168]{2,1,0:T(8,128)(2,1)} %wd_ref.1, bf16[2,7168,128]{2,1,0:T(8,128)(2,1)} %wu_ref.1, f32[2,128,128]{2,1,0:T(8,128)S(1)} %fusion.36, bf16[2,128,3072]{2,1,0:T(8,128)(2,1)S(1)} %bitcast.79, bf16[2,128,4096]{2,1,0:T(8,128)(2,1)} %bitcast.81), kind=kOutput, calls=%fused_computation.23 | convolution fusion | flops 947060736 | bytes 18481152 | tf_op jit(solution)/shard_map/eck,ekn->ecn/dot_general | solution.py:445
  130.9 9.7 %fusion.1 = bf16[2,128,7168]{2,1,0:T(8,128)(2,1)} fusion(f32[2,128,7168]{2,1,0:T(8,128)} %fusion.8, bf16[2,128,7168]{2,1,0:T(8,128)(2,1)} %get-tuple-element.22, f32[2,128]{1,0:T(2,128)S(1)} %mul.56, bf16[2,7168,128]{2,1,0:T(8,128)(2,1)} %get-tuple-element.21, f32[2,128,128]{2,1,0:T(8,128)S(1)} %fusion.35, bf16[2,128,3072]{2,1,0:T(8,128)(2,1)S(1)} %bitcast.80, ...), kind=kOutput, calls=%fused_computation.2 | convolution fusion | flops 952565760 | bytes 22152192 | tf_op jit(solution)/shard_map/eck,ekn->ecn/dot_general | solution.py:445
  140.7 3.3 %slice.12 = bf16[2,128,4096]{2,1,0:T(8,128)(2,1)} slice(bf16[2,128,7168]{2,1,0:T(8,128)(2,1)} %fusion.1), slice={[0:2], [0:128], [0:4096]} | slice | bytes 4194304 | tf_op jit(solution)/shard_map/slice | solution.py:452
  143.9 2.7 convolution_convert_fusion.3
  146.6 66.0 %line_sum_and_plane.1 = (bf16[2,32,4096]{2,1,0:T(8,128)(2,1)}, bf16[16,32,3072]{2,1,0:T(8,128)(2,1)}) custom-call(bf16[2,4,32,4096]{3,2,1,0:T(8,128)(2,1)} %bitcast.85, bf16[16,32,3072]{2,1,0:T(8,128)(2,1)} %bitcast.75), custom_call_target="tpu_custom_call" | custom-call | tf_op jit(solution)/shard_map/line_sum_and_plane/pallas_call | solution.py:314
  212.7 4.1 %convolution_convert_fusion.5 = bf16[256,3072]{1,0:T(8,128)(2,1)} fusion(pred[512,256]{1,0:T(32,128)(4,1)S(1)} %and.165, bf16[512,3072]{1,0:T(8,128)(2,1)} %bitcast.88), kind=kOutput, calls=%fused_computation.15 | convolution fusion | flops 806092800 | bytes 4849664 | tf_op jit(solution)/shard_map/dot_general | solution.py:386
  216.8 1.4 fusion.3.blk_ref
  218.2 30.8 %ring_sum_and_plane.1 = (bf16[32,3072]{1,0:T(8,128)(2,1)}, bf16[16,8,4096]{2,1,0:T(8,128)(2,1)}) custom-call(bf16[8,32,3072]{2,1,0:T(8,128)(2,1)} %bitcast.86, bf16[16,8,4096]{2,1,0:T(8,128)(2,1)} %fusion.3.blk_ref), custom_call_target="tpu_custom_call" | custom-call | tf_op jit(solution)/shard_map/ring_sum_and_plane/pallas_call | solution.py:375
  249.1 2.2 convolution_convert_fusion.2.own_ref
  251.3 13.7 %pair_exchange.3 = bf16[32,4096]{1,0:T(8,128)(2,1)} custom-call(bf16[32,4096]{1,0:T(8,128)(2,1)} %convolution_convert_fusion.2.own_ref), custom_call_target="tpu_custom_call" | custom-call | tf_op jit(solution)/shard_map/pair_exchange/pallas_call | solution.py:89
  264.9 1.5 fusion.5
  266.5 1.7 pad_maximum_fusion.1
  (45 shorter events, 6.9 us)
Async XLA Ops:
  0.0 31.4 %copy-start.2 = (bf16[32,7168]{1,0:T(8,128)(2,1)S(1)}, bf16[32,7168]{1,0:T(8,128)(2,1)}, u32[]{:S(2)}) copy-start(bf16[32,7168]{1,0:T(8,128)(2,1)} %tok_ref.1) | copy-start | bytes 1376260
  114.3 3.1 %copy-start = (bf16[2,4,32,4096]{3,2,1,0:T(8,128)(2,1)S(1)}, bf16[2,4,32,4096]{3,2,1,0:T(8,128)(2,1)}, u32[]{:S(2)}) copy-start(bf16[2,4,32,4096]{3,2,1,0:T(8,128)(2,1)} %get-tuple-element.18) | copy-start | bytes 6291460
  117.4 3.4 %copy-start.1 = (bf16[2,7168,128]{2,1,0:T(8,128)(2,1)S(1)}, bf16[2,7168,128]{2,1,0:T(8,128)(2,1)}, u32[]{:S(2)}) copy-start(bf16[2,7168,128]{2,1,0:T(8,128)(2,1)} %wg_ref.1) | copy-start | bytes 11010052
  140.7 3.3 %slice-start = ((bf16[2,128,7168]{2,1,0:T(8,128)(2,1)}), bf16[2,128,3072]{2,1,0:T(8,128)(2,1)S(1)}, s32[]{:S(2)}) async-start(bf16[2,128,7168]{2,1,0:T(8,128)(2,1)} %fusion.1), calls=%async_computation | async-start | bytes 3145728 | tf_op jit(solution)/shard_map/slice | solution.py:453
  212.6 4.2 %copy-start.3 = (bf16[2,32,4096]{2,1,0:T(8,128)(2,1)S(1)}, bf16[2,32,4096]{2,1,0:T(8,128)(2,1)}, u32[]{:S(2)}) copy-start(bf16[2,32,4096]{2,1,0:T(8,128)(2,1)} %get-tuple-element.24) | copy-start | bytes 1572868

commit v2 on v1

--- a/solution.py
+++ b/solution.py
@@ -11,6 +11,7 @@
 COLS = NX * NY
 D1 = 4096
 SLOTS = 4
+XY_ORDER = ((2, 2), (1, 1), (3, 3), (1, 3), (3, 1), (2, 1), (1, 2), (2, 3), (3, 2), (2, 0), (0, 2), (1, 0), (3, 0), (0, 1), (0, 3))
 BF = jnp.bfloat16
 F32 = jnp.float32
 ANY = pl.BlockSpec(memory_space=pl.ANY)
@@ -38,10 +39,7 @@
 
 def xy_targets():
     x, y = lax.axis_index("x"), lax.axis_index("y")
-    found = []
-    for d in range(1, COLS):
-        found.append((lax.rem(x + d // NY, NX), lax.rem(y + d % NY, NY)))
-    return found
+    return [(lax.rem(x + dx, NX), lax.rem(y + dy, NY)) for dx, dy in XY_ORDER]
 
 
 def xy_devices():
@@ -96,48 +94,48 @@
     )(own)
 
 
+def sub(q, rows, width, first=0):
+    half, wide = rows // 2, width // 2
+    return pl.ds(q // 2 * half, half), pl.ds(first + q % 2 * wide, wide)
+
+
+RING_HOPS = [(t, q, up) for t in range(NZ // 2) for q in range(4) for up in (True, False)]
+
+
 def ring_kernel(tok_ref, blk_ref, all_ref, got_ref, xs, xr, us, ur, ds, dr, ls):
     z = my_z()
-    rows = tok_ref.shape[0]
-    half = rows // 2
-    width = all_ref.shape[2]
+    _, rows, width = all_ref.shape
     start_col = tok_ref.shape[1] - width
     greet(xy_devices() + [z_of(z + 1), z_of(z - 1)])
     me = lax.axis_index("x") * NY + lax.axis_index("y")
-
-    def hop(t, h, up):
-        who = lax.rem(z + (-(t - 1) if up else t - 1) + NZ, NZ)
-        part = pl.ds(h * half, half)
-        if t == 1:
-            src = tok_ref.at[part, pl.ds(start_col, width)]
-        else:
-            src = all_ref.at[who, part]
+    last = NZ // 2 - 1
+
+    def hop(t, q, up):
+        who = lax.rem(z + (-t if up else t) + NZ, NZ)
+        r, c = sub(q, rows, width)
+        src = tok_ref.at[sub(q, rows, width, start_col)] if t == 0 else all_ref.at[who, r, c]
         send, recv = (us, ur) if up else (ds, dr)
-        return remote(src, all_ref.at[who, part], send.at[t - 1, h], recv.at[t - 1, h], z_of(z + (1 if up else -1)))
-
-    last = NZ // 2
-    hops = [(t, h, up) for t in range(1, last + 1) for h in range(2) for up in (True, False)
-            if t < last or (h == 0) == up]
-    for t, h, up in hops:
-        if t == 1:
-            hop(t, h, up).start()
+        return remote(src, all_ref.at[who, r, c], send.at[t, q], recv.at[t, q], z_of(z + (1 if up else -1)))
+
+    hops = [(t, q, up) for t, q, up in RING_HOPS if t < last or (q < 2) == up]
+    for t, q, up in hops:
+        if t == 0:
+            hop(t, q, up).start()
     blocks = xy_copies(blk_ref, got_ref, xs, xr)
     for copy in blocks:
         copy.start()
-    own = [pltpu.make_async_copy(tok_ref.at[:, pl.ds(start_col, width)], all_ref.at[z], ls.at[0]),
-           pltpu.make_async_copy(blk_ref.at[me], got_ref.at[me], ls.at[1])]
-    for copy in own:
-        copy.start()
-    for t, h, up in hops:
-        hop(t, h, up).wait_recv()
-        if (t + 1, h, up) in hops:
-            hop(t + 1, h, up).start()
-    for t, h, up in hops:
-        hop(t, h, up).wait_send()
+    own = pltpu.make_async_copy(blk_ref.at[me], got_ref.at[me], ls)
+    own.start()
+    all_ref[z] = tok_ref[:, start_col:]
+    for t, q, up in hops:
+        hop(t, q, up).wait_recv()
+        if (t + 1, q, up) in hops:
+            hop(t + 1, q, up).start()
+    for t, q, up in hops:
+        hop(t, q, up).wait_send()
     for copy in blocks:
         copy.wait()
-    for copy in own:
-        copy.wait()
+    own.wait()
 
 
 def ring_and_plane(tokens, blocks, cid):
@@ -146,8 +144,8 @@
     return pl.pallas_call(
         ring_kernel,
         out_shape=(jax.ShapeDtypeStruct((NZ, rows, width), BF), jax.ShapeDtypeStruct(blocks.shape, BF)),
-        in_specs=[ANY, ANY], out_specs=(ANY, ANY),
-        scratch_shapes=[DMA((COLS - 1,)), DMA((COLS - 1,))] + [DMA((NZ // 2, 2))] * 4 + [DMA((2,))],
+        in_specs=[VMEM, ANY], out_specs=(VMEM, ANY),
+        scratch_shapes=[DMA((COLS - 1,)), DMA((COLS - 1,))] + [DMA((NZ // 2, 4))] * 4 + [DMA],
         compiler_params=pltpu.CompilerParams(collective_id=cid, has_side_effects=True),
         name="ring_and_plane",
     )(tokens, blocks)
@@ -252,36 +250,52 @@
         return remote(src, buf.at[slot, e], send.at[slot, e], recv.at[slot, e], {"zl": above if up else below})
 
     order = [(NL - 1 - i, i) for i in range(NL - 1)]
-    for ju, jd in order:
-        for e in range(experts):
-            @pl.when(zl == 0)
-            def _():
-                hop(ju, e, True, True).start()
-
-            @pl.when(zl == NL - 1)
-            def _():
-                hop(jd, e, False, True).start()
     blocks = xy_copies(blk_ref, got_ref, xs, xr)
     for copy in blocks:
         copy.start()
     own = pltpu.make_async_copy(blk_ref.at[me], got_ref.at[me], ls)
     own.start()
+    edge = [(i, e) for i in range(NL - 1) for e in range(experts)]
+    for up, home in ((True, 0), (False, NL - 1)):
+        @pl.when(zl == home)
+        def _():
+            copies = [hop(NL - 1 - i if up else i, e, up, True) for i, e in edge]
+            copies[0].start()
+            copies[1].start()
+            for n in range(2, len(copies)):
+                copies[n - 2].wait_send()
+                copies[n].start()
+            copies[-2].wait_send()
+            copies[-1].wait_send()
+
+    def pass_on(j, e, up):
+        slot = j - 1 if up else j
+        buf = ub if up else db
+        copy = hop(j, e, up, False)
+        copy.wait_recv()
+        add_into(buf.at[slot, e], buf.at[slot, e], part_ref.at[e, j], width)
+        copy.start()
+
+    for home, near in ((1, True), (2, False)):
+        far, mid = (3, 2) if near else (0, 1)
+        back = 0 if near else 3
+        events = [(far, 0, near), (far, 1, near), (back, 0, not near), (mid, 0, near), (back, 1, not near), (mid, 1, near)]
+
+        @pl.when(zl == home)
+        def _():
+            for event in events:
+                pass_on(*event)
+            for j, e, up in events:
+                hop(j, e, up, False).wait_send()
     for ju, jd in order:
         for e in range(experts):
-            for up, j in ((True, ju), (False, jd)):
-                inner = (zl > 0) & (zl <= j) if up else (zl < NL - 1) & (zl >= j)
-                passes = (zl > 0) & (zl < j) if up else (zl < NL - 1) & (zl > j)
-                slot = j - 1 if up else j
-                buf = ub if up else db
-
-                @pl.when(inner)
-                def _():
-                    hop(j, e, up, False).wait_recv()
-
-                @pl.when(passes)
-                def _():
-                    add_into(buf.at[slot, e], buf.at[slot, e], part_ref.at[e, j], width)
-                    hop(j, e, up, False).start()
+            @pl.when(zl == ju)
+            def _():
+                hop(ju, e, True, False).wait_recv()
+
+            @pl.when(zl == jd)
+            def _():
+                hop(jd, e, False, False).wait_recv()
     for e in range(experts):
         @pl.when(zl == 0)
         def _():
@@ -294,15 +308,6 @@
             @pl.when(zl == mid)
             def _():
                 add_into(out_ref.at[e], part_ref.at[e, mid], ub.at[mid - 1, e], width, db.at[mid, e])
-    for ju, jd in order:
-        for e in range(experts):
-            @pl.when(zl < ju)
-            def _():
-                hop(ju, e, True, False).wait_send()
-
-            @pl.when(zl > jd)
-            def _():
-                hop(jd, e, False, False).wait_send()
     for copy in blocks:
         copy.wait()
     own.wait()
@@ -324,7 +329,7 @@
 def ring_sum_kernel(part_ref, blk_ref, out_ref, got_ref, ub, db, xs, xr, us, ur, ds, dr, ls):
     z = my_z()
     rows, width = out_ref.shape
-    half = rows // 2
+    wide = width // 2
     me = lax.axis_index("x") * NY + lax.axis_index("y")
     greet(xy_devices() + [z_of(z + 1), z_of(z - 1)])
     last = NZ // 2
@@ -332,38 +337,35 @@
     def spot(t, up):
         return lax.rem(z + (last - t if up else t - last) + NZ, NZ)
 
-    def rows_of(h):
-        return pl.ds(h * half, half)
-
-    def hop(t, h, up, fresh):
+    def hop(t, q, up, fresh):
         buf = ub if up else db
         send, recv = (us, ur) if up else (ds, dr)
-        src = part_ref.at[spot(t, up), rows_of(h)] if fresh else buf.at[t - 1, h]
-        return remote(src, buf.at[t, h], send.at[t, h], recv.at[t, h], z_of(z + (1 if up else -1)))
-
-    def fresh_of(t, h, up):
-        return t == 0 or (t == 1 and (h == 0) != up)
-
-    hops = [(t, h, up) for t in range(last) for h in range(2) for up in (True, False)
-            if t > 0 or (h == 0) == up]
-    for t, h, up in hops:
-        if fresh_of(t, h, up):
-            hop(t, h, up, True).start()
+        src = part_ref.at[(spot(t, up),) + sub(q, rows, width)] if fresh else buf.at[t - 1, q]
+        return remote(src, buf.at[t, q], send.at[t, q], recv.at[t, q], z_of(z + (1 if up else -1)))
+
+    def fresh_of(t, q, up):
+        return t == 0 or (t == 1 and (q < 2) != up)
+
+    hops = [(t, q, up) for t, q, up in RING_HOPS if t > 0 or (q < 2) == up]
+    for t, q, up in hops:
+        if fresh_of(t, q, up):
+            hop(t, q, up, True).start()
     blocks = xy_copies(blk_ref, got_ref, xs, xr)
     for copy in blocks:
         copy.start()
     own = pltpu.make_async_copy(blk_ref.at[me], got_ref.at[me], ls)
     own.start()
-    for t, h, up in hops:
+    for t, q, up in hops:
         buf = ub if up else db
-        hop(t, h, up, fresh_of(t, h, up)).wait_recv()
+        hop(t, q, up, fresh_of(t, q, up)).wait_recv()
         if t < last - 1:
-            add_into(buf.at[t, h], buf.at[t, h], part_ref.at[spot(t + 1, up), rows_of(h)], width)
-            hop(t + 1, h, up, False).start()
-    for h in range(2):
-        add_into(out_ref.at[rows_of(h)], part_ref.at[z, rows_of(h)], ub.at[last - 1, h], width, db.at[last - 1, h])
-    for t, h, up in hops:
-        hop(t, h, up, fresh_of(t, h, up)).wait_send()
+            add_into(buf.at[t, q], buf.at[t, q], part_ref.at[(spot(t + 1, up),) + sub(q, rows, width)], wide)
+            hop(t + 1, q, up, False).start()
+    for q in range(4):
+        where = sub(q, rows, width)
+        add_into(out_ref.at[where], part_ref.at[(z,) + where], ub.at[last - 1, q], wide, db.at[last - 1, q])
+    for t, q, up in hops:
+        hop(t, q, up, fresh_of(t, q, up)).wait_send()
     for copy in blocks:
         copy.wait()
     own.wait()
@@ -371,15 +373,122 @@
 
 def ring_sum_and_plane(parts, blocks, cid):
     _, rows, width = parts.shape
-    buf = pltpu.VMEM((NZ // 2, 2, rows // 2, width), BF)
+    buf = pltpu.VMEM((NZ // 2, 4, rows // 2, width // 2), BF)
     return pl.pallas_call(
         ring_sum_kernel,
         out_shape=(jax.ShapeDtypeStruct((rows, width), BF), jax.ShapeDtypeStruct(blocks.shape, BF)),
         in_specs=[VMEM, ANY], out_specs=(VMEM, ANY),
-        scratch_shapes=[buf, buf, DMA((COLS - 1,)), DMA((COLS - 1,))] + [DMA((NZ // 2, 2))] * 4 + [DMA],
+        scratch_shapes=[buf, buf, DMA((COLS - 1,)), DMA((COLS - 1,))] + [DMA((NZ // 2, 4))] * 4 + [DMA],
         compiler_params=pltpu.CompilerParams(collective_id=cid, has_side_effects=True),
         name="ring_sum_and_plane",
     )(parts, blocks)
+
+
+CHUNK = 1024
+NEAR = D1 // CHUNK
+
+
+def hidden_kernel(x1_ref, got_ref, fit_ref, g0_ref, g1_ref, u0_ref, u1_ref, h_ref, acc):
+    d = pl.program_id(0)
+    experts, rows, half = h_ref.shape
+
+    @pl.when(d == 0)
+    def _():
+        acc[...] = jnp.zeros(acc.shape, F32)
+
+    def add(e, x):
+        both = jnp.concatenate([g0_ref[e], g1_ref[e], u0_ref[e], u1_ref[e]], axis=1)
+        acc[e] += jnp.dot(x, both, preferred_element_type=F32)
+
+    @pl.when(d < NEAR)
+    def _():
+        for e in range(experts):
+            add(e, x1_ref[e])
+
+    @pl.when(d >= NEAR)
+    def _():
+        for e in range(experts):
+            fit = fit_ref[e * rows:(e + 1) * rows, :]
+            add(e, jnp.dot(fit, got_ref[...], preferred_element_type=F32).astype(BF))
+
+    @pl.when(d == pl.num_programs(0) - 1)
+    def _():
+        for e in range(experts):
+            gate, up = acc[e, :, :half], acc[e, :, half:]
+            h_ref[e] = (gate / (1.0 + jnp.exp(-gate)) * up).astype(BF)
+
+
+def hidden_of(x1, got2, fit2, g0, g1, u0, u1):
+    experts, rows, _ = x1.shape
+    width, cols = g0.shape[1], g0.shape[2]
+    weight = pl.BlockSpec((experts, CHUNK, cols), lambda d: (0, d, 0))
+    return pl.pallas_call(
+        hidden_kernel,
+        grid=(width // CHUNK,),
+        out_shape=jax.ShapeDtypeStruct((experts, rows, 2 * cols), BF),
+        in_specs=[
+            pl.BlockSpec((experts, rows, CHUNK), lambda d: (0, 0, jnp.minimum(d, NEAR - 1))),
+            pl.BlockSpec((got2.shape[0], CHUNK), lambda d: (0, jnp.maximum(d - NEAR, 0))),
+            pl.BlockSpec(fit2.shape, lambda d: (0, 0)),
+            weight, weight, weight, weight],
+        out_specs=pl.BlockSpec((experts, rows, 2 * cols), lambda d: (0, 0, 0)),
+        scratch_shapes=[pltpu.VMEM((experts, rows, 4 * cols), F32)],
+        compiler_params=pltpu.CompilerParams(dimension_semantics=("arbitrary",)),
+        name="hidden_units",
+    )(x1, got2, fit2, g0, g1, u0, u1)
+
+
+def down_kernel(h_ref, fit_ref, wt_ref, d0_ref, d1_ref, near_ref, far_ref, padded, scale):
+    d = pl.program_id(0)
+    experts, rows, units = h_ref.shape
+    turn = (((0,), (0,)), ((), ()))
+
+    @pl.when(d == 0)
+    def _():
+        scale[...] = jnp.zeros(scale.shape, F32)
+        for e in range(experts):
+            fit = fit_ref[e * rows:(e + 1) * rows, :]
+            placed = lax.dot_general(fit, h_ref[e], turn, preferred_element_type=F32)
+            padded[:, e * units:(e + 1) * units] = placed.astype(BF)
+            wide = jnp.broadcast_to(wt_ref[e], (rows, scale.shape[1]))
+            scale[...] += lax.dot_general(fit.astype(F32), wide, turn, precision=lax.Precision.HIGHEST,
+                                          preferred_element_type=F32)
+
+    @pl.when(d < NEAR)
+    def _():
+        for e in range(experts):
+            both = jnp.concatenate([d0_ref[e], d1_ref[e]], axis=0)
+            y = jnp.dot(h_ref[e], both, preferred_element_type=F32)
+            near_ref[e] = (y * wt_ref[e]).astype(BF)
+
+    @pl.when(d >= NEAR)
+    def _():
+        both = jnp.concatenate([ref[e] for e in range(experts) for ref in (d0_ref, d1_ref)], axis=0)
+        y = jnp.dot(padded[...], both, preferred_element_type=F32)
+        far_ref[...] = (y * scale[:, :1]).astype(BF)
+
+
+def down_of(hidden, fit2, weight, d0, d1):
+    experts, rows, units = hidden.shape
+    cols, width = d0.shape[1], d0.shape[2]
+    slots = fit2.shape[1]
+    mat = pl.BlockSpec((experts, cols, CHUNK), lambda d: (0, 0, d))
+    return pl.pallas_call(
+        down_kernel,
+        grid=(width // CHUNK,),
+        out_shape=(jax.ShapeDtypeStruct((experts, rows, D1), BF), jax.ShapeDtypeStruct((slots, width - D1), BF)),
+        in_specs=[
+            pl.BlockSpec(hidden.shape, lambda d: (0, 0, 0)),
+            pl.BlockSpec(fit2.shape, lambda d: (0, 0)),
+            pl.BlockSpec((experts, rows, 1), lambda d: (0, 0, 0)),
+            mat, mat],
+        out_specs=(
+            pl.BlockSpec((experts, rows, CHUNK), lambda d: (0, 0, jnp.minimum(d, NEAR - 1))),
+            pl.BlockSpec((slots, CHUNK), lambda d: (0, jnp.maximum(d - NEAR, 0)))),
+        scratch_shapes=[pltpu.VMEM((slots, experts * units), BF), pltpu.VMEM((slots, 128), F32)],
+        compiler_params=pltpu.CompilerParams(dimension_semantics=("arbitrary",)),
+        name="down_units",
+    )(hidden, fit2, weight, d0, d1)
 
 
 def mm(a, b, dtype=BF):
@@ -438,19 +547,9 @@
     lines, got2, og, ou, od = line_and_plane(
         rows1, out2.reshape(COLS, NL * experts * SLOTS, width - D1), w_gate, w_up, w_down, 3)
     x1 = lines.reshape(experts, NL * cap, D1)
-    x2 = mm(fit2, got2.reshape(-1, width - D1)).reshape(experts, NL * cap, width - D1)
-    chosen = jnp.concatenate([x1, x2], axis=2)
-
-    def einsum(a, b):
-        return jnp.einsum("eck,ekn->ecn", a, b, preferred_element_type=F32)
-
-    down = 0.0
-    for g, u, d in ((w_gate, w_up, w_down), (og, ou, od)):
-        hidden = (jax.nn.silu(einsum(chosen, g)) * einsum(chosen, u)).astype(BF)
-        down = down + einsum(hidden, d)
-    partial = (down * weight).astype(BF)
-    back1 = partial[:, :, :D1].reshape(experts, NL, cap, D1)
-    back2 = mm(fit2.T, partial[:, :, D1:].reshape(experts * NL * cap, width - D1))
+    hidden = hidden_of(x1, got2.reshape(-1, width - D1), fit2, w_gate, og, w_up, ou)
+    back1, back2 = down_of(hidden, fit2, weight, w_down, od)
+    back1 = back1.reshape(experts, NL, cap, D1)
     summed, home2 = line_sum_and_plane(back1, back2.reshape(COLS, NL * experts * SLOTS, width - D1), 4)
     give1 = mm(fit1.T, summed.reshape(experts * cap, D1))
     sums2 = mm(pick2.T, home2.reshape(-1, width - D1)).reshape(NZ, rows, width - D1)

time: 271 us -> 231 us (0.85)
  matrix products: 47.6 us -> 19.6 us
  Pallas kernels: 203 us -> 194 us
    dot_general x4 -> x0, matrix products: 23.2 us -> none  [einsum(): return jnp.einsum('eck,ekn->ecn', a, b, preferred_element_type=F32)]
    pallas_call x1, Pallas kernels: 66 us -> 43.7 us  [line_sum_and_plane(): pl.pallas_call(line_sum_kernel, out_shape=(jax.ShapeDtypeStruct((experts,...]
    pallas_call x0 -> x2, Pallas kernels: none -> 20.9 us  [the longest x1 10.9 us: hidden_of(): pl.pallas_call(hidden_kernel, grid=(width // CHUNK,), out_shape=jax.Shape...]
    pallas_call x1, Pallas kernels: 45 us -> 37.2 us  [line_and_plane(): pl.pallas_call(line_kernel, out_shape=tuple((jax.ShapeDtypeStruct(s, BF)...]
    dot_general x10 -> x8, matrix products: 24.4 us -> 19.6 us  [mm(): return jnp.dot(a, b, preferred_element_type=F32).astype(dtype)]
    slice x3 -> x0, local copies, waits for them, and re-layouts: 3.28 us -> none  [the longest x1 3.28 us: body(): back1 = partial[:, :, :D1].reshape(experts, NL, cap, D1)]
    pallas_call x2, Pallas kernels: 32.4 us -> 35.3 us  [pair_exchange(): pl.pallas_call(pair_kernel, out_shape=jax.ShapeDtypeStruct((rows, width),...]
where the time goes in v2:
time: 231 us; the launch traced here: 228 us
  Pallas kernels  194 us (84%)
  matrix products  19.6 us (8%)
  other arithmetic  8.32 us (4%)
  local copies, waits for them, and re-layouts  5.3 us (2%)
    pallas_call x1, Pallas kernels, line_sum_and_plane(): pl.pallas_call(line_sum_kernel, out_shape=(jax.ShapeDtypeStruct((experts,...  43.7 us
    pallas_call x1, Pallas kernels, line_and_plane(): pl.pallas_call(line_kernel, out_shape=tuple((jax.ShapeDtypeStruct(s, BF)...  37.2 us
    pallas_call x2, Pallas kernels, pair_exchange(): pl.pallas_call(pair_kernel, out_shape=jax.ShapeDtypeStruct((rows, width),...  35.3 us
    pallas_call x1, Pallas kernels, ring_sum_and_plane(): pl.pallas_call(ring_sum_kernel, out_shape=(jax.ShapeDtypeStruct((rows, wi...  29 us
    pallas_call x1, Pallas kernels, ring_and_plane(): pl.pallas_call(ring_kernel, out_shape=(jax.ShapeDtypeStruct((NZ, rows, wi...  28.4 us
    dot_general x8, matrix products, mm(): return jnp.dot(a, b, preferred_element_type=F32).astype(dtype)  19.6 us
    pallas_call x1, Pallas kernels, hidden_of(): pl.pallas_call(hidden_kernel, grid=(width // CHUNK,), out_shape=jax.Shape...  10.9 us
    pallas_call x1, Pallas kernels, down_of(): pl.pallas_call(down_kernel, grid=(width // CHUNK,), out_shape=(jax.ShapeD...  10 us

profile of v2, /device:TPU:64, one launch (start us, length us, event | category | flops | bytes accessed | tf_op | source)
XLA Modules:
  0.0 228.0 jit_solution(17074596836726320795)
XLA Ops:
  0.0 1.0 copy.52
  1.3 3.0 %convert_reduce_fusion = s32[4,16,2,32]{3,2,1,0:T(2,128)S(1)} fusion(s32[4,16,2,32]{3,2,1,0:T(2,128)S(1)} %and_select_fusion.1, pred[32,32]{1,0:T(8,128)(4,1)S(1)} %iota_compare_fusion), kind=kLoop, calls=%fused_computation.12 | loop fusion | flops 520192 | bytes 33792 | tf_op jit(solution)/shard_map/reduce_sum | solution.py:515
  4.5 1.8 compare_reduce_fusion
  6.7 1.4 fusion.7
  8.3 19.6 %pair_exchange.2 = bf16[32,4096]{1,0:T(8,128)(2,1)} custom-call(bf16[32,7168]{1,0:T(8,128)(2,1)} %tok_ref.1), custom_call_target="tpu_custom_call" | custom-call | tf_op jit(solution)/shard_map/pair_exchange/pallas_call | solution.py:87
  27.9 2.4 %fusion.2.blk_ref = bf16[16,8,4096]{2,1,0:T(8,128)(2,1)} fusion(f32[128,4096]{1,0:T(8,128)S(1)} %fusion.7, bf16[32,4096]{1,0:T(8,128)(2,1)} %pair_exchange.2, pred[128,1,32]{0,2,1:T(32,128)(4,1)S(1)} %copy.64), kind=kOutput, calls=%fused_computation.5 | convolution fusion | flops 34603008 | bytes 3411968 | tf_op jit(solution)/shard_map/dot_general | solution.py:495
  30.3 28.4 %ring_and_plane.1 = (bf16[8,32,3072]{2,1,0:T(8,128)(2,1)}, bf16[16,8,4096]{2,1,0:T(8,128)(2,1)}) custom-call(bf16[32,7168]{1,0:T(8,128)(2,1)} %tok_ref.1, bf16[16,8,4096]{2,1,0:T(8,128)(2,1)} %fusion.2.blk_ref), custom_call_target="tpu_custom_call" | custom-call | tf_op jit(solution)/shard_map/ring_and_plane/pallas_call | solution.py:144
  59.0 1.0 broadcast_and_fusion
  60.0 0.7 and.153
  60.7 4.3 %convolution_convert_fusion.3 = bf16[512,3072]{1,0:T(8,128)(2,1)} fusion(pred[512,256]{1,0:T(32,128)(4,1)S(1)} %and.153, bf16[256,3072]{1,0:T(8,128)(2,1)} %bitcast.70), kind=kOutput, calls=%fused_computation.10 | convolution fusion | flops 806879232 | bytes 4849664 | tf_op jit(solution)/shard_map/dot_general | solution.py:495
  65.5 1.2 convolution_convert_fusion.1
  66.6 37.2 %line_and_plane.1 = (bf16[2,4,32,4096]{3,2,1,0:T(8,128)(2,1)}, bf16[16,32,3072]{2,1,0:T(8,128)(2,1)}, bf16[2,7168,128]{2,1,0:T(8,128)(2,1)}, bf16[2,7168,128]{2,1,0:T(8,128)(2,1)}, bf16[2,128,7168]{2,1,0:T(8,128)(2,1)}) custom-call(bf16[2,32,4096]{2,1,0:T(8,128)(2,1)} %bitcast.68, bf16[16,32,3072]{2,1,0:T(8,128)(2,1)} %bitcast.62, ...), custom_call_target="tpu_custom_call" | custom-call | tf_op jit(solution)/shard_map/line_and_plane/pallas_call | solution.py:216
  105.7 0.8 copy.66.fit_ref
  106.5 10.9 %hidden_units.1.h_ref = bf16[2,128,256]{2,1,0:T(8,128)(2,1)} custom-call(bf16[2,128,4096]{2,1,0:T(8,128)(2,1)} %bitcast.67, bf16[512,3072]{1,0:T(8,128)(2,1)} %bitcast.64, bf16[256,512]{1,0:T(8,128)(2,1)} %copy.66.fit_ref, bf16[2,7168,128]{2,1,0:T(8,128)(2,1)} %g0_ref.1, bf16[2,7168,128]{2,1,0:T(8,128)(2,1)} %get-tuple-element.22.g1_ref, ...), custom_call_target="tpu_custom_call" | custom-call | tf_op jit(solution)/shard_map/hidden_units/pallas_call | solution.py:425
  117.6 0.8 reshape.330.wt_ref
  118.4 10.0 %down_units.1 = (bf16[2,128,4096]{2,1,0:T(8,128)(2,1)}, bf16[512,3072]{1,0:T(8,128)(2,1)}) custom-call(bf16[2,128,256]{2,1,0:T(8,128)(2,1)} %hidden_units.1.h_ref, bf16[256,512]{1,0:T(8,128)(2,1)} %copy.66.fit_ref, f32[2,128,1]{2,1,0:T(8,128)} %reshape.330.wt_ref, bf16[2,128,7168]{2,1,0:T(8,128)(2,1)} %d0_ref.1, bf16[2,128,7168]{2,1,0:T(8,128)(2,1)} %get-tuple-element.24.d1_ref), custom_call_target="tpu_custom_call" | custom-call | tf_op jit(solution)/shard_map/down_units/pallas_call | solution.py:476
  128.4 43.7 %line_sum_and_plane.1 = (bf16[2,32,4096]{2,1,0:T(8,128)(2,1)}, bf16[16,32,3072]{2,1,0:T(8,128)(2,1)}) custom-call(bf16[2,4,32,4096]{3,2,1,0:T(8,128)(2,1)} %bitcast.69, bf16[16,32,3072]{2,1,0:T(8,128)(2,1)} %bitcast.65), custom_call_target="tpu_custom_call" | custom-call | tf_op jit(solution)/shard_map/line_sum_and_plane/pallas_call | solution.py:319
  172.1 2.5 %fusion.1.blk_ref = bf16[16,8,4096]{2,1,0:T(8,128)(2,1)} fusion(pred[64,128]{0,1:T(32,128)(4,1)S(1)} %and.158, bf16[64,4096]{1,0:T(8,128)(2,1)} %bitcast.73), kind=kOutput, calls=%fused_computation.4 | convolution fusion | flops 67633152 | bytes 1581056 | tf_op jit(solution)/shard_map/dot_general | solution.py:495
  174.6 4.1 %convolution_convert_fusion.4 = bf16[256,3072]{1,0:T(8,128)(2,1)} fusion(pred[512,256]{1,0:T(32,128)(4,1)S(1)} %and.153, bf16[512,3072]{1,0:T(8,128)(2,1)} %bitcast.66), kind=kOutput, calls=%fused_computation.11 | convolution fusion | flops 806092800 | bytes 4849664 | tf_op jit(solution)/shard_map/dot_general | solution.py:495
  178.7 29.0 %ring_sum_and_plane.1 = (bf16[32,3072]{1,0:T(8,128)(2,1)}, bf16[16,8,4096]{2,1,0:T(8,128)(2,1)}) custom-call(bf16[8,32,3072]{2,1,0:T(8,128)(2,1)} %bitcast.63, bf16[16,8,4096]{2,1,0:T(8,128)(2,1)} %fusion.1.blk_ref), custom_call_target="tpu_custom_call" | custom-call | tf_op jit(solution)/shard_map/ring_sum_and_plane/pallas_call | solution.py:377
  207.7 2.2 convolution_convert_fusion.2.own_ref
  209.9 15.7 %pair_exchange.3 = bf16[32,4096]{1,0:T(8,128)(2,1)} custom-call(bf16[32,4096]{1,0:T(8,128)(2,1)} %convolution_convert_fusion.2.own_ref), custom_call_target="tpu_custom_call" | custom-call | tf_op jit(solution)/shard_map/pair_exchange/pallas_call | solution.py:87
  225.7 1.5 fusion.3
  227.2 0.8 pad_maximum_fusion
  (37 shorter events, 3.7 us)
Async XLA Ops:
  60.7 4.7 %copy-start = (bf16[16,8,4096]{2,1,0:T(8,128)(2,1)S(1)}, bf16[16,8,4096]{2,1,0:T(8,128)(2,1)}, u32[]{:S(2)}) copy-start(bf16[16,8,4096]{2,1,0:T(8,128)(2,1)} %get-tuple-element.18) | copy-start | bytes 3145732
  106.5 10.9 %copy-start.2 = (f32[8,64,32]{1,2,0:T(8,128)S(1)}, f32[8,64,32]{1,2,0:T(8,128)}, u32[]{:S(2)}) copy-start(f32[8,64,32]{1,2,0:T(8,128)} %param.10) | copy-start | bytes 196612
  207.7 19.5 %copy-start.1 = (bf16[32,3072]{1,0:T(8,128)(2,1)S(1)}, bf16[32,3072]{1,0:T(8,128)(2,1)}, u32[]{:S(2)}) copy-start(bf16[32,3072]{1,0:T(8,128)(2,1)} %get-tuple-element.30) | copy-start | bytes 589828

commit v3 on v2

--- a/solution.py
+++ b/solution.py
@@ -11,6 +11,8 @@
 COLS = NX * NY
 D1 = 4096
 SLOTS = 4
+CHUNK = 1024
+NEAR = D1 // CHUNK
 XY_ORDER = ((2, 2), (1, 1), (3, 3), (1, 3), (3, 1), (2, 1), (1, 2), (2, 3), (3, 2), (2, 0), (0, 2), (1, 0), (3, 0), (0, 1), (0, 3))
 BF = jnp.bfloat16
 F32 = jnp.float32
@@ -58,40 +60,16 @@
     return lax.axis_index("zh") * NL + lax.axis_index("zl")
 
 
-def pair_kernel(own_ref, out_ref, relay, send, recv):
+def pair_steps(src, relay, dst, send, recv):
     z = my_z()
-    rows, width = out_ref.shape
-    half = rows // 2
-    greet([z_of(z + 2), z_of(z - 2)])
-    first = []
+    half = relay.shape[1]
+    first, second = [], []
     for d, step in enumerate((2, -2)):
         part = pl.ds(d * half, half)
-        copy = remote(own_ref.at[part, pl.ds(0, width)], relay.at[d], send.at[d], recv.at[d], z_of(z + step))
-        copy.start()
-        first.append(copy)
-    second = []
-    for d, step in enumerate((2, -2)):
-        part = pl.ds(d * half, half)
-        first[d].wait_recv()
-        copy = remote(relay.at[d], out_ref.at[part], send.at[2 + d], recv.at[2 + d], z_of(z + step))
-        copy.start()
-        second.append(copy)
-    for copy in first:
-        copy.wait_send()
-    for copy in second:
-        copy.wait()
-
-
-def pair_exchange(own, width, cid):
-    rows = own.shape[0]
-    return pl.pallas_call(
-        pair_kernel,
-        out_shape=jax.ShapeDtypeStruct((rows, width), BF),
-        in_specs=[ANY], out_specs=ANY,
-        scratch_shapes=[pltpu.VMEM((2, rows // 2, width), BF), DMA((4,)), DMA((4,))],
-        compiler_params=pltpu.CompilerParams(collective_id=cid, has_side_effects=True),
-        name="pair_exchange",
-    )(own)
+        near = z_of(z + step)
+        first.append(remote(src.at[part, pl.ds(0, relay.shape[2])], relay.at[d], send.at[d], recv.at[d], near))
+        second.append(remote(relay.at[d], dst.at[part], send.at[2 + d], recv.at[2 + d], near))
+    return first, second
 
 
 def sub(q, rows, width, first=0):
@@ -102,11 +80,13 @@
 RING_HOPS = [(t, q, up) for t in range(NZ // 2) for q in range(4) for up in (True, False)]
 
 
-def ring_kernel(tok_ref, blk_ref, all_ref, got_ref, xs, xr, us, ur, ds, dr, ls):
+def head_kernel(tok_ref, mine_ref, theirs_ref, all_ref, got_ref, other, relay, block,
+                xs, xr, us, ur, ds, dr, ps, pr, ls):
     z = my_z()
     _, rows, width = all_ref.shape
+    cols, wide = block.shape[0], block.shape[2]
     start_col = tok_ref.shape[1] - width
-    greet(xy_devices() + [z_of(z + 1), z_of(z - 1)])
+    greet(xy_devices() + [z_of(z + 1), z_of(z - 1), z_of(z + 2), z_of(z - 2)])
     me = lax.axis_index("x") * NY + lax.axis_index("y")
     last = NZ // 2 - 1
 
@@ -118,37 +98,64 @@
         return remote(src, all_ref.at[who, r, c], send.at[t, q], recv.at[t, q], z_of(z + (1 if up else -1)))
 
     hops = [(t, q, up) for t, q, up in RING_HOPS if t < last or (q < 2) == up]
+
+    def serve(step):
+        for t, q, up in hops:
+            if t == step:
+                hop(t, q, up).wait_recv()
+                if (t + 1, q, up) in hops:
+                    hop(t + 1, q, up).start()
+
+    first, second = pair_steps(tok_ref, relay, other, ps, pr)
+    for copy in first:
+        copy.start()
     for t, q, up in hops:
         if t == 0:
             hop(t, q, up).start()
-    blocks = xy_copies(blk_ref, got_ref, xs, xr)
-    for copy in blocks:
-        copy.start()
-    own = pltpu.make_async_copy(blk_ref.at[me], got_ref.at[me], ls)
+    all_ref[z] = tok_ref[:, start_col:]
+    for d in range(2):
+        first[d].wait_recv()
+        second[d].start()
+    serve(0)
+    for copy in second:
+        copy.wait_recv()
+
+    @pl.loop(0, wide // CHUNK)
+    def _(i):
+        part = pl.ds(pl.multiple_of(i * CHUNK, CHUNK), CHUNK)
+        y = jnp.dot(mine_ref[...], tok_ref[:, part], preferred_element_type=F32)
+        y = y + jnp.dot(theirs_ref[...], other[:, part], preferred_element_type=F32)
+        block[:, :, part] = y.reshape(cols, y.shape[0] // cols, CHUNK).astype(BF)
+
+    blocks = xy_copies(block, got_ref, xs, xr)
+    for copy in blocks:
+        copy.start()
+    own = pltpu.make_async_copy(block.at[me], got_ref.at[me], ls)
     own.start()
-    all_ref[z] = tok_ref[:, start_col:]
-    for t, q, up in hops:
-        hop(t, q, up).wait_recv()
-        if (t + 1, q, up) in hops:
-            hop(t + 1, q, up).start()
+    for step in range(1, last + 1):
+        serve(step)
     for t, q, up in hops:
         hop(t, q, up).wait_send()
+    for copy in first + second:
+        copy.wait_send()
     for copy in blocks:
         copy.wait()
     own.wait()
 
 
-def ring_and_plane(tokens, blocks, cid):
+def head(tokens, mine, theirs, cid):
     rows = tokens.shape[0]
     width = tokens.shape[1] - D1
+    block = (COLS, mine.shape[0] // COLS, D1)
     return pl.pallas_call(
-        ring_kernel,
-        out_shape=(jax.ShapeDtypeStruct((NZ, rows, width), BF), jax.ShapeDtypeStruct(blocks.shape, BF)),
-        in_specs=[VMEM, ANY], out_specs=(VMEM, ANY),
-        scratch_shapes=[DMA((COLS - 1,)), DMA((COLS - 1,))] + [DMA((NZ // 2, 4))] * 4 + [DMA],
+        head_kernel,
+        out_shape=(jax.ShapeDtypeStruct((NZ, rows, width), BF), jax.ShapeDtypeStruct(block, BF)),
+        in_specs=[VMEM, VMEM, VMEM], out_specs=(VMEM, ANY),
+        scratch_shapes=[pltpu.VMEM((rows, D1), BF), pltpu.VMEM((2, rows // 2, D1), BF), pltpu.VMEM(block, BF),
+                        DMA((COLS - 1,)), DMA((COLS - 1,))] + [DMA((NZ // 2, 4))] * 4 + [DMA((4,)), DMA((4,)), DMA],
         compiler_params=pltpu.CompilerParams(collective_id=cid, has_side_effects=True),
-        name="ring_and_plane",
-    )(tokens, blocks)
+        name="head",
+    )(tokens, mine, theirs)
 
 
 def line_kernel(row_ref, blk_ref, wg_ref, wu_ref, wd_ref, all_ref, got_ref, og_ref, ou_ref, od_ref,
@@ -326,12 +333,14 @@
     )(parts, blocks)
 
 
-def ring_sum_kernel(part_ref, blk_ref, out_ref, got_ref, ub, db, xs, xr, us, ur, ds, dr, ls):
+def tail_kernel(part_ref, blk_ref, mine_ref, theirs_ref, out_ref, home, away, own, got, relay, ub, db,
+                xs, xr, us, ur, ds, dr, ps, pr, ls):
     z = my_z()
-    rows, width = out_ref.shape
+    _, rows, width = part_ref.shape
+    near = own.shape[1]
     wide = width // 2
     me = lax.axis_index("x") * NY + lax.axis_index("y")
-    greet(xy_devices() + [z_of(z + 1), z_of(z - 1)])
+    greet(xy_devices() + [z_of(z + 1), z_of(z - 1), z_of(z + 2), z_of(z - 2)])
     last = NZ // 2
 
     def spot(t, up):
@@ -347,45 +356,73 @@
         return t == 0 or (t == 1 and (q < 2) != up)
 
     hops = [(t, q, up) for t, q, up in RING_HOPS if t > 0 or (q < 2) == up]
+
+    def serve(step):
+        for t, q, up in hops:
+            if t == step:
+                buf = ub if up else db
+                hop(t, q, up, fresh_of(t, q, up)).wait_recv()
+                if t < last - 1:
+                    add_into(buf.at[t, q], buf.at[t, q], part_ref.at[(spot(t + 1, up),) + sub(q, rows, width)], wide)
+                    hop(t + 1, q, up, False).start()
+
     for t, q, up in hops:
         if fresh_of(t, q, up):
             hop(t, q, up, True).start()
-    blocks = xy_copies(blk_ref, got_ref, xs, xr)
-    for copy in blocks:
-        copy.start()
-    own = pltpu.make_async_copy(blk_ref.at[me], got_ref.at[me], ls)
-    own.start()
-    for t, q, up in hops:
-        buf = ub if up else db
-        hop(t, q, up, fresh_of(t, q, up)).wait_recv()
-        if t < last - 1:
-            add_into(buf.at[t, q], buf.at[t, q], part_ref.at[(spot(t + 1, up),) + sub(q, rows, width)], wide)
-            hop(t + 1, q, up, False).start()
+    blocks = xy_copies(blk_ref, home, xs, xr)
+    for copy in blocks:
+        copy.start()
+    keep = pltpu.make_async_copy(blk_ref.at[me], home.at[me], ls)
+    keep.start()
+    serve(0)
+    serve(1)
+    for copy in blocks:
+        copy.wait_recv()
+    keep.wait()
+    turn = (((0,), (0,)), ((), ()))
+
+    @pl.loop(0, near // CHUNK)
+    def _(i):
+        part = pl.ds(pl.multiple_of(i * CHUNK, CHUNK), CHUNK)
+        h = home[:, :, part].astype(F32).reshape(mine_ref.shape[0], CHUNK).astype(BF)
+        away[:, part] = lax.dot_general(theirs_ref[...], h, turn, preferred_element_type=F32).astype(BF)
+        own[:, part] = lax.dot_general(mine_ref[...], h, turn, preferred_element_type=F32)
+
+    first, second = pair_steps(away, relay, got, ps, pr)
+    for copy in first:
+        copy.start()
+    serve(2)
+    for d in range(2):
+        first[d].wait_recv()
+        second[d].start()
+    serve(3)
     for q in range(4):
-        where = sub(q, rows, width)
-        add_into(out_ref.at[where], part_ref.at[(z,) + where], ub.at[last - 1, q], wide, db.at[last - 1, q])
+        r, c = sub(q, rows, width)
+        there = out_ref.at[sub(q, rows, width, near)]
+        add_into(there, part_ref.at[z, r, c], ub.at[last - 1, q], wide, db.at[last - 1, q])
+    for copy in second:
+        copy.wait_recv()
+    add_into(out_ref.at[:, pl.ds(0, near)], own, got, near)
     for t, q, up in hops:
         hop(t, q, up, fresh_of(t, q, up)).wait_send()
-    for copy in blocks:
-        copy.wait()
-    own.wait()
-
-
-def ring_sum_and_plane(parts, blocks, cid):
+    for copy in first + second + blocks:
+        copy.wait_send()
+
+
+def tail(parts, blocks, mine, theirs, cid):
     _, rows, width = parts.shape
+    near = blocks.shape[2]
     buf = pltpu.VMEM((NZ // 2, 4, rows // 2, width // 2), BF)
     return pl.pallas_call(
-        ring_sum_kernel,
-        out_shape=(jax.ShapeDtypeStruct((rows, width), BF), jax.ShapeDtypeStruct(blocks.shape, BF)),
-        in_specs=[VMEM, ANY], out_specs=(VMEM, ANY),
-        scratch_shapes=[buf, buf, DMA((COLS - 1,)), DMA((COLS - 1,))] + [DMA((NZ // 2, 4))] * 4 + [DMA],
+        tail_kernel,
+        out_shape=jax.ShapeDtypeStruct((rows, near + width), BF),
+        in_specs=[VMEM, ANY, VMEM, VMEM], out_specs=VMEM,
+        scratch_shapes=[pltpu.VMEM(blocks.shape, BF), pltpu.VMEM((rows, near), BF), pltpu.VMEM((rows, near), F32),
+                        pltpu.VMEM((rows, near), BF), pltpu.VMEM((2, rows // 2, near), BF), buf, buf,
+                        DMA((COLS - 1,)), DMA((COLS - 1,))] + [DMA((NZ // 2, 4))] * 4 + [DMA((4,)), DMA((4,)), DMA],
         compiler_params=pltpu.CompilerParams(collective_id=cid, has_side_effects=True),
-        name="ring_sum_and_plane",
-    )(parts, blocks)
-
-
-CHUNK = 1024
-NEAR = D1 // CHUNK
+        name="tail",
+    )(parts, blocks, mine, theirs)
 
 
 def hidden_kernel(x1_ref, got_ref, fit_ref, g0_ref, g1_ref, u0_ref, u1_ref, h_ref, acc):
@@ -537,11 +574,9 @@
     weight = lax.dynamic_index_in_dim(of_parity(gates), col, 1, keepdims=False)
     weight = weight.transpose(1, 0, 2).reshape(experts, NL * cap, 1)
 
-    other = pair_exchange(tokens, D1, 1)
     pick_own = lax.dynamic_index_in_dim(pick1, zh, 1, keepdims=False)
     pick_other = lax.dynamic_index_in_dim(pick1, 1 - zh, 1, keepdims=False)
-    out1 = (mm(pick_own, tokens[:, :D1], F32) + mm(pick_other, other, F32)).astype(BF)
-    everyone, got1 = ring_and_plane(tokens, out1.reshape(COLS, experts * SLOTS, D1), 2)
+    everyone, got1 = head(tokens, pick_own, pick_other, 1)
     rows1 = mm(fit1, got1.reshape(-1, D1)).reshape(experts, cap, D1)
     out2 = mm(pick2, everyone.reshape(NZ * rows, width - D1))
     lines, got2, og, ou, od = line_and_plane(
@@ -553,11 +588,7 @@
     summed, home2 = line_sum_and_plane(back1, back2.reshape(COLS, NL * experts * SLOTS, width - D1), 4)
     give1 = mm(fit1.T, summed.reshape(experts * cap, D1))
     sums2 = mm(pick2.T, home2.reshape(-1, width - D1)).reshape(NZ, rows, width - D1)
-    final2, home1 = ring_sum_and_plane(sums2, give1.reshape(COLS, experts * SLOTS, D1), 5)
-    home1 = home1.reshape(-1, D1)
-    returned = pair_exchange(mm(pick_other.T, home1), D1, 6)
-    final1 = (mm(pick_own.T, home1, F32) + returned.astype(F32)).astype(BF)
-    return jnp.concatenate([final1, final2], axis=1)
+    return tail(sums2, give1.reshape(COLS, experts * SLOTS, D1), pick_own, pick_other, 2)
 
 
 def solution(mesh):

time: 231 us -> 219 us (0.948)
  matrix products: 19.6 us -> 12 us
  Pallas kernels: 194 us -> 189 us
    pallas_call x4 -> x2, Pallas kernels: 92.7 us -> 83.3 us  [the longest x1 42.6 us: head(): pl.pallas_call(head_kernel, out_shape=(jax.ShapeDtypeStruct((NZ, rows, wi...]
    dot_general x8 -> x4, matrix products: 19.6 us -> 12 us  [mm(): return jnp.dot(a, b, preferred_element_type=F32).astype(dtype)]
    pallas_call x1, Pallas kernels: 37.2 us -> 41.2 us  [line_and_plane(): pl.pallas_call(line_kernel, out_shape=tuple((jax.ShapeDtypeStruct(s, BF)...]
where the time goes in v3:
time: 219 us; the launch traced here: 216 us
  Pallas kernels  189 us (86%)
  matrix products  12 us (5%)
  other arithmetic  7.54 us (3%)
  local copies, waits for them, and re-layouts  7.51 us (3%)
    pallas_call x1, Pallas kernels, line_sum_and_plane(): pl.pallas_call(line_sum_kernel, out_shape=(jax.ShapeDtypeStruct((experts,...  43.7 us
    pallas_call x1, Pallas kernels, head(): pl.pallas_call(head_kernel, out_shape=(jax.ShapeDtypeStruct((NZ, rows, wi...  42.6 us
    pallas_call x1, Pallas kernels, line_and_plane(): pl.pallas_call(line_kernel, out_shape=tuple((jax.ShapeDtypeStruct(s, BF)...  41.2 us
    pallas_call x1, Pallas kernels, tail(): pl.pallas_call(tail_kernel, out_shape=jax.ShapeDtypeStruct((rows, near +...  40.6 us
    dot_general x4, matrix products, mm(): return jnp.dot(a, b, preferred_element_type=F32).astype(dtype)  12 us
    pallas_call x1, Pallas kernels, hidden_of(): pl.pallas_call(hidden_kernel, grid=(width // CHUNK,), out_shape=jax.Shape...  10.8 us
    pallas_call x1, Pallas kernels, down_of(): pl.pallas_call(down_kernel, grid=(width // CHUNK,), out_shape=(jax.ShapeD...  10.2 us

profile of v3, /device:TPU:64, one launch (start us, length us, event | category | flops | bytes accessed | tf_op | source)
XLA Modules:
  0.0 216.4 jit_solution(6140237060128140007)
XLA Ops:
  0.0 1.0 copy.54
  1.3 3.0 %convert_reduce_fusion = s32[4,16,2,32]{3,2,1,0:T(2,128)S(1)} fusion(s32[4,16,2,32]{3,2,1,0:T(2,128)S(1)} %and_select_fusion.1, pred[32,32]{1,0:T(8,128)(4,1)S(1)} %iota_compare_fusion), kind=kLoop, calls=%fused_computation.6 | loop fusion | flops 520192 | bytes 33792 | tf_op jit(solution)/shard_map/reduce_sum | solution.py:552
  4.2 0.3 compare_select_fusion
  4.5 1.8 compare_reduce_fusion
  6.6 0.6 copy_bitcast_fusion.1
  7.2 42.6 %head.1 = (bf16[8,32,3072]{2,1,0:T(8,128)(2,1)}, bf16[16,8,4096]{2,1,0:T(8,128)(2,1)}) custom-call(bf16[32,7168]{1,0:T(8,128)(2,1)} %tok_ref.1, bf16[128,32]{1,0:T(8,128)(2,1)} %get-tuple-element.30.mine_ref, bf16[128,32]{1,0:T(8,128)(2,1)} %get-tuple-element.29.theirs_ref), custom_call_target="tpu_custom_call" | custom-call | tf_op jit(solution)/shard_map/head/pallas_call | solution.py:150
  49.9 0.2 reshape.321
  50.2 1.0 broadcast_and_fusion
  51.2 0.7 and.153
  52.0 4.2 %convolution_convert_fusion.2 = bf16[512,3072]{1,0:T(8,128)(2,1)} fusion(pred[512,256]{1,0:T(32,128)(4,1)S(1)} %and.153, bf16[256,3072]{1,0:T(8,128)(2,1)} %bitcast.60), kind=kOutput, calls=%fused_computation.4 | convolution fusion | flops 806879232 | bytes 4849664 | tf_op jit(solution)/shard_map/dot_general | solution.py:532
  56.7 1.2 convolution_convert_fusion.1
  57.8 41.2 %line_and_plane.1 = (bf16[2,4,32,4096]{3,2,1,0:T(8,128)(2,1)}, bf16[16,32,3072]{2,1,0:T(8,128)(2,1)}, bf16[2,7168,128]{2,1,0:T(8,128)(2,1)}, bf16[2,7168,128]{2,1,0:T(8,128)(2,1)}, bf16[2,128,7168]{2,1,0:T(8,128)(2,1)}) custom-call(bf16[2,32,4096]{2,1,0:T(8,128)(2,1)} %bitcast.58, bf16[16,32,3072]{2,1,0:T(8,128)(2,1)} %bitcast.52, ...), custom_call_target="tpu_custom_call" | custom-call | tf_op jit(solution)/shard_map/line_and_plane/pallas_call | solution.py:223
  99.1 0.4 broadcast_and_fusion.1
  99.5 0.7 and_convert_fusion
  100.2 0.7 reshape.320
  100.9 0.8 copy.70.fit_ref
  101.8 10.8 %hidden_units.1.h_ref = bf16[2,128,256]{2,1,0:T(8,128)(2,1)} custom-call(bf16[2,128,4096]{2,1,0:T(8,128)(2,1)} %bitcast.57, bf16[512,3072]{1,0:T(8,128)(2,1)} %bitcast.54, bf16[256,512]{1,0:T(8,128)(2,1)} %copy.70.fit_ref, bf16[2,7168,128]{2,1,0:T(8,128)(2,1)} %g0_ref.1, bf16[2,7168,128]{2,1,0:T(8,128)(2,1)} %get-tuple-element.20.g1_ref, ...), custom_call_target="tpu_custom_call" | custom-call | tf_op jit(solution)/shard_map/hidden_units/pallas_call | solution.py:462
  112.7 0.8 reshape.322.wt_ref
  113.5 10.2 %down_units.1 = (bf16[2,128,4096]{2,1,0:T(8,128)(2,1)}, bf16[512,3072]{1,0:T(8,128)(2,1)}) custom-call(bf16[2,128,256]{2,1,0:T(8,128)(2,1)} %hidden_units.1.h_ref, bf16[256,512]{1,0:T(8,128)(2,1)} %copy.70.fit_ref, f32[2,128,1]{2,1,0:T(8,128)} %reshape.322.wt_ref, bf16[2,128,7168]{2,1,0:T(8,128)(2,1)} %d0_ref.1, bf16[2,128,7168]{2,1,0:T(8,128)(2,1)} %get-tuple-element.22.d1_ref), custom_call_target="tpu_custom_call" | custom-call | tf_op jit(solution)/shard_map/down_units/pallas_call | solution.py:513
  123.7 43.7 %line_sum_and_plane.1 = (bf16[2,32,4096]{2,1,0:T(8,128)(2,1)}, bf16[16,32,3072]{2,1,0:T(8,128)(2,1)}) custom-call(bf16[2,4,32,4096]{3,2,1,0:T(8,128)(2,1)} %bitcast.59, bf16[16,32,3072]{2,1,0:T(8,128)(2,1)} %bitcast.55), custom_call_target="tpu_custom_call" | custom-call | tf_op jit(solution)/shard_map/line_sum_and_plane/pallas_call | solution.py:326
  167.4 2.5 %fusion.blk_ref = bf16[16,8,4096]{2,1,0:T(8,128)(2,1)} fusion(pred[64,128]{0,1:T(32,128)(4,1)S(1)} %and.158, bf16[64,4096]{1,0:T(8,128)(2,1)} %bitcast.63), kind=kOutput, calls=%fused_computation.2 | convolution fusion | flops 67633152 | bytes 1581056 | tf_op jit(solution)/shard_map/dot_general | solution.py:532
  169.9 4.1 %convolution_convert_fusion.3 = bf16[256,3072]{1,0:T(8,128)(2,1)} fusion(pred[512,256]{1,0:T(32,128)(4,1)S(1)} %and.153, bf16[512,3072]{1,0:T(8,128)(2,1)} %bitcast.56), kind=kOutput, calls=%fused_computation.5 | convolution fusion | flops 806092800 | bytes 4849664 | tf_op jit(solution)/shard_map/dot_general | solution.py:532
  174.0 40.6 %tail.1 = bf16[32,7168]{1,0:T(8,128)(2,1)} custom-call(bf16[8,32,3072]{2,1,0:T(8,128)(2,1)} %bitcast.53, bf16[16,8,4096]{2,1,0:T(8,128)(2,1)} %fusion.blk_ref, bf16[128,32]{1,0:T(8,128)(2,1)} %get-tuple-element.30.mine_ref, bf16[128,32]{1,0:T(8,128)(2,1)} %get-tuple-element.29.theirs_ref), custom_call_target="tpu_custom_call" | custom-call | tf_op jit(solution)/shard_map/tail/pallas_call | solution.py:416
  214.6 1.8 copy.111
  (28 shorter events, 1.2 us)
Async XLA Ops:
  52.0 4.7 %copy-start = (bf16[16,8,4096]{2,1,0:T(8,128)(2,1)S(1)}, bf16[16,8,4096]{2,1,0:T(8,128)(2,1)}, u32[]{:S(2)}) copy-start(bf16[16,8,4096]{2,1,0:T(8,128)(2,1)} %get-tuple-element.16) | copy-start | bytes 3145732
  101.8 10.8 %copy-start.1 = (f32[8,64,32]{1,2,0:T(8,128)S(1)}, f32[8,64,32]{1,2,0:T(8,128)}, u32[]{:S(2)}) copy-start(f32[8,64,32]{1,2,0:T(8,128)} %param.10) | copy-start | bytes 196612

commit v4 on v3

--- a/solution.py
+++ b/solution.py
@@ -12,6 +12,7 @@
 D1 = 4096
 SLOTS = 4
 CHUNK = 1024
+HALF = 512
 NEAR = D1 // CHUNK
 XY_ORDER = ((2, 2), (1, 1), (3, 3), (1, 3), (3, 1), (2, 1), (1, 2), (2, 3), (3, 2), (2, 0), (0, 2), (1, 0), (3, 0), (0, 1), (0, 3))
 BF = jnp.bfloat16
@@ -80,22 +81,27 @@
 RING_HOPS = [(t, q, up) for t in range(NZ // 2) for q in range(4) for up in (True, False)]
 
 
-def head_kernel(tok_ref, mine_ref, theirs_ref, all_ref, got_ref, other, relay, block,
-                xs, xr, us, ur, ds, dr, ps, pr, ls):
+def front_kernel(tok_ref, mine_ref, theirs_ref, pick_ref, fit_ref, wg_ref, wu_ref, wd_ref,
+                 line_ref, got_ref, og_ref, ou_ref, od_ref,
+                 ring, other, relay, block, home, far,
+                 xs, xr, ys, yr, us, ur, ds, dr, ps, pr, lus, lur, lds, ldr, ws, wr, ls):
     z = my_z()
-    _, rows, width = all_ref.shape
+    zl = lax.axis_index("zl")
+    experts = line_ref.shape[0]
+    _, rows, width = ring.shape
     cols, wide = block.shape[0], block.shape[2]
     start_col = tok_ref.shape[1] - width
-    greet(xy_devices() + [z_of(z + 1), z_of(z - 1), z_of(z + 2), z_of(z - 2)])
+    core = {"c": 1 - lax.axis_index("c")}
+    greet(xy_devices() + [z_of(z + 1), z_of(z - 1), z_of(z + 2), z_of(z - 2), core])
     me = lax.axis_index("x") * NY + lax.axis_index("y")
     last = NZ // 2 - 1
 
     def hop(t, q, up):
         who = lax.rem(z + (-t if up else t) + NZ, NZ)
         r, c = sub(q, rows, width)
-        src = tok_ref.at[sub(q, rows, width, start_col)] if t == 0 else all_ref.at[who, r, c]
+        src = tok_ref.at[sub(q, rows, width, start_col)] if t == 0 else ring.at[who, r, c]
         send, recv = (us, ur) if up else (ds, dr)
-        return remote(src, all_ref.at[who, r, c], send.at[t, q], recv.at[t, q], z_of(z + (1 if up else -1)))
+        return remote(src, ring.at[who, r, c], send.at[t, q], recv.at[t, q], z_of(z + (1 if up else -1)))
 
     hops = [(t, q, up) for t, q, up in RING_HOPS if t < last or (q < 2) == up]
 
@@ -106,13 +112,29 @@
                 if (t + 1, q, up) in hops:
                     hop(t + 1, q, up).start()
 
+    def pass_on(i, e, up):
+        who = lax.rem(zl + (-i if up else i) + NL, NL)
+        send, recv = (lus, lur) if up else (lds, ldr)
+        place = line_ref.at[e, who]
+        return remote(place, place, send.at[i, e], recv.at[i, e], z_of(z + (1 if up else -1)))
+
+    def sends(i, up):
+        return (zl < NL - 1) & (zl >= i) if up else (zl > 0) & (zl + i < NL)
+
+    def gets(i, up):
+        return zl - 1 - i >= 0 if up else zl + 1 + i < NL
+
     first, second = pair_steps(tok_ref, relay, other, ps, pr)
     for copy in first:
         copy.start()
     for t, q, up in hops:
         if t == 0:
             hop(t, q, up).start()
-    all_ref[z] = tok_ref[:, start_col:]
+    weights = [remote(a, b, ws.at[i], wr.at[i], core)
+               for i, (a, b) in enumerate(((wg_ref, og_ref), (wu_ref, ou_ref), (wd_ref, od_ref)))]
+    for copy in weights:
+        copy.start()
+    ring[z] = tok_ref[:, start_col:]
     for d in range(2):
         first[d].wait_recv()
         second[d].start()
@@ -127,108 +149,87 @@
         y = y + jnp.dot(theirs_ref[...], other[:, part], preferred_element_type=F32)
         block[:, :, part] = y.reshape(cols, y.shape[0] // cols, CHUNK).astype(BF)
 
-    blocks = xy_copies(block, got_ref, xs, xr)
+    blocks = xy_copies(block, home, xs, xr)
     for copy in blocks:
         copy.start()
-    own = pltpu.make_async_copy(block.at[me], got_ref.at[me], ls)
-    own.start()
+    home[me] = block[me]
     for step in range(1, last + 1):
         serve(step)
-    for t, q, up in hops:
-        hop(t, q, up).wait_send()
-    for copy in first + second:
-        copy.wait_send()
     for copy in blocks:
-        copy.wait()
-    own.wait()
-
-
-def head(tokens, mine, theirs, cid):
-    rows = tokens.shape[0]
-    width = tokens.shape[1] - D1
-    block = (COLS, mine.shape[0] // COLS, D1)
-    return pl.pallas_call(
-        head_kernel,
-        out_shape=(jax.ShapeDtypeStruct((NZ, rows, width), BF), jax.ShapeDtypeStruct(block, BF)),
-        in_specs=[VMEM, VMEM, VMEM], out_specs=(VMEM, ANY),
-        scratch_shapes=[pltpu.VMEM((rows, D1), BF), pltpu.VMEM((2, rows // 2, D1), BF), pltpu.VMEM(block, BF),
-                        DMA((COLS - 1,)), DMA((COLS - 1,))] + [DMA((NZ // 2, 4))] * 4 + [DMA((4,)), DMA((4,)), DMA],
-        compiler_params=pltpu.CompilerParams(collective_id=cid, has_side_effects=True),
-        name="head",
-    )(tokens, mine, theirs)
-
-
-def line_kernel(row_ref, blk_ref, wg_ref, wu_ref, wd_ref, all_ref, got_ref, og_ref, ou_ref, od_ref,
-                xs, xr, us, ur, ds, dr, ws, wr, ls):
-    zl = lax.axis_index("zl")
-    experts = row_ref.shape[0]
-    me = lax.axis_index("x") * NY + lax.axis_index("y")
-    above, below = lax.rem(zl + 1, NL), lax.rem(zl + NL - 1, NL)
-    other = {"c": 1 - lax.axis_index("c")}
-    greet(xy_devices() + [{"zl": above}, {"zl": below}, other])
-
-    def hop(i, e, up):
-        who = lax.rem(zl + (-i if up else i) + NL, NL)
-        src = row_ref.at[e] if i == 0 else all_ref.at[e, who]
-        send, recv = (us, ur) if up else (ds, dr)
-        return remote(src, all_ref.at[e, who], send.at[i, e], recv.at[i, e], {"zl": above if up else below})
-
-    def sends(i, up):
-        return (zl < NL - 1) & (zl >= i) if up else (zl > 0) & (zl + i < NL)
-
-    def gets(i, up):
-        return zl - 1 - i >= 0 if up else zl + 1 + i < NL
+        copy.wait_recv()
+
+    @pl.loop(0, wide // CHUNK)
+    def _(i):
+        part = pl.ds(pl.multiple_of(i * CHUNK, CHUNK), CHUNK)
+        h = home[:, :, part].astype(F32).reshape(fit_ref.shape[1], CHUNK).astype(BF)
+        y = jnp.dot(fit_ref[...], h, preferred_element_type=F32).astype(BF)
+        cap = y.shape[0] // experts
+        for e in range(experts):
+            line_ref[e, zl, :, part] = y[e * cap:(e + 1) * cap]
 
     for e in range(experts):
         for up in (True, False):
             @pl.when(sends(0, up))
             def _():
-                hop(0, e, up).start()
-    blocks = xy_copies(blk_ref, got_ref, xs, xr)
-    for copy in blocks:
-        copy.start()
-    weights = [remote(a, b, ws.at[i], wr.at[i], other)
-               for i, (a, b) in enumerate(((wg_ref, og_ref), (wu_ref, ou_ref), (wd_ref, od_ref)))]
-    for copy in weights:
-        copy.start()
-    own = [pltpu.make_async_copy(row_ref.at[e], all_ref.at[e, zl], ls.at[e]) for e in range(experts)]
-    own.append(pltpu.make_async_copy(blk_ref.at[me], got_ref.at[me], ls.at[experts]))
-    for copy in own:
-        copy.start()
+                pass_on(0, e, up).start()
+
+    @pl.loop(0, width // HALF)
+    def _(i):
+        part = pl.ds(pl.multiple_of(i * HALF, HALF), HALF)
+        every = ring[:, :, part].reshape(NZ * rows, HALF)
+        y = jnp.dot(pick_ref[...], every, preferred_element_type=F32)
+        far[:, :, part] = y.reshape(cols, y.shape[0] // cols, HALF).astype(BF)
+
+    fars = xy_copies(far, got_ref, ys, yr)
+    for copy in fars:
+        copy.start()
+    own = pltpu.make_async_copy(far.at[me], got_ref.at[me], ls)
+    own.start()
     for i in range(NL - 1):
         for e in range(experts):
             for up in (True, False):
                 @pl.when(gets(i, up))
                 def _():
-                    hop(i, e, up).wait_recv()
+                    pass_on(i, e, up).wait_recv()
                 if i < NL - 2:
                     @pl.when(sends(i + 1, up))
                     def _():
-                        hop(i + 1, e, up).start()
+                        pass_on(i + 1, e, up).start()
     for i in range(NL - 1):
         for e in range(experts):
             for up in (True, False):
                 @pl.when(sends(i, up))
                 def _():
-                    hop(i, e, up).wait_send()
-    for copy in blocks + weights:
+                    pass_on(i, e, up).wait_send()
+    for t, q, up in hops:
+        hop(t, q, up).wait_send()
+    for copy in first + second + blocks:
+        copy.wait_send()
+    for copy in fars + weights:
         copy.wait()
-    for copy in own:
-        copy.wait()
-
-
-def line_and_plane(rows, blocks, w_gate, w_up, w_down, cid):
-    experts, cap, width = rows.shape
-    shapes = [(experts, NL, cap, width), blocks.shape, w_gate.shape, w_up.shape, w_down.shape]
+    own.wait()
+
+
+def front(tokens, mine, theirs, pick2, fit1, w_gate, w_up, w_down, cid):
+    rows = tokens.shape[0]
+    width = tokens.shape[1] - D1
+    experts = w_gate.shape[0]
+    cap = fit1.shape[0] // experts
+    block = (COLS, mine.shape[0] // COLS, D1)
+    far = (COLS, pick2.shape[0] // COLS, width)
+    shapes = [(experts, NL, cap, D1), far, w_gate.shape, w_up.shape, w_down.shape]
+    plane = DMA((COLS - 1,))
     return pl.pallas_call(
-        line_kernel,
-        out_shape=tuple(jax.ShapeDtypeStruct(s, BF) for s in shapes),
-        in_specs=[ANY] * 5, out_specs=(ANY,) * 5,
-        scratch_shapes=[DMA((COLS - 1,)), DMA((COLS - 1,))] + [DMA((NL - 1, experts))] * 4
-        + [DMA((3,)), DMA((3,)), DMA((experts + 1,))],
+        front_kernel,
+        out_shape=tuple(jax.ShapeDtypeStruct(shape, BF) for shape in shapes),
+        in_specs=[VMEM] * 5 + [ANY] * 3, out_specs=(VMEM, ANY, ANY, ANY, ANY),
+        scratch_shapes=[pltpu.VMEM((NZ, rows, width), BF), pltpu.VMEM((rows, D1), BF),
+                        pltpu.VMEM((2, rows // 2, D1), BF), pltpu.VMEM(block, BF), pltpu.VMEM(block, BF),
+                        pltpu.VMEM(far, BF), plane, plane, plane, plane]
+        + [DMA((NZ // 2, 4))] * 4 + [DMA((4,))] * 2 + [DMA((NL - 1, experts))] * 4 + [DMA((3,))] * 2 + [DMA],
         compiler_params=pltpu.CompilerParams(collective_id=cid, has_side_effects=True),
-        name="line_and_plane",
-    )(rows, blocks, w_gate, w_up, w_down)
+        name="front",
+    )(tokens, mine, theirs, pick2, fit1, w_gate, w_up, w_down)
 
 
 def add_into(dst, a, b, width, extra=None, chunk=512):
@@ -241,32 +242,39 @@
         dst[:, part] = total.astype(BF)
 
 
-def line_sum_kernel(part_ref, blk_ref, out_ref, got_ref, ub, db, xs, xr, us, ur, ds, dr, ls):
+def back_kernel(line_ref, far_ref, mine_ref, theirs_ref, pick_ref, fit_ref, out_ref,
+                lu, ld, summed, got2, part_ref, block, home, away, own, got, relay, ub, db,
+                xs, xr, ys, yr, us, ur, ds, dr, ps, pr, lus, lur, lds, ldr, ls):
+    z = my_z()
     zl = lax.axis_index("zl")
-    experts = part_ref.shape[0]
-    width = part_ref.shape[3]
+    experts = line_ref.shape[0]
+    near = line_ref.shape[3]
+    _, rows, width = part_ref.shape
+    wide = width // 2
+    cols = block.shape[0]
     me = lax.axis_index("x") * NY + lax.axis_index("y")
-    above, below = lax.rem(zl + 1, NL), lax.rem(zl + NL - 1, NL)
-    greet(xy_devices() + [{"zl": above}, {"zl": below}])
-
-    def hop(j, e, up, fresh):
-        buf = ub if up else db
+    greet(xy_devices() + [z_of(z + 1), z_of(z - 1), z_of(z + 2), z_of(z - 2)])
+    last = NZ // 2
+    turn = (((0,), (0,)), ((), ()))
+
+    def send_sum(j, e, up, fresh):
+        buf = lu if up else ld
         slot = j - 1 if up else j
-        send, recv = (us, ur) if up else (ds, dr)
-        src = part_ref.at[e, j] if fresh else buf.at[slot, e]
-        return remote(src, buf.at[slot, e], send.at[slot, e], recv.at[slot, e], {"zl": above if up else below})
+        send, recv = (lus, lur) if up else (lds, ldr)
+        src = line_ref.at[e, j] if fresh else buf.at[slot, e]
+        return remote(src, buf.at[slot, e], send.at[slot, e], recv.at[slot, e], z_of(z + (1 if up else -1)))
 
     order = [(NL - 1 - i, i) for i in range(NL - 1)]
-    blocks = xy_copies(blk_ref, got_ref, xs, xr)
-    for copy in blocks:
-        copy.start()
-    own = pltpu.make_async_copy(blk_ref.at[me], got_ref.at[me], ls)
-    own.start()
+    fars = xy_copies(far_ref, got2, ys, yr)
+    for copy in fars:
+        copy.start()
+    keep = pltpu.make_async_copy(far_ref.at[me], got2.at[me], ls)
+    keep.start()
     edge = [(i, e) for i in range(NL - 1) for e in range(experts)]
-    for up, home in ((True, 0), (False, NL - 1)):
-        @pl.when(zl == home)
+    for up, seat in ((True, 0), (False, NL - 1)):
+        @pl.when(zl == seat)
         def _():
-            copies = [hop(NL - 1 - i if up else i, e, up, True) for i, e in edge]
+            copies = [send_sum(NL - 1 - i if up else i, e, up, True) for i, e in edge]
             copies[0].start()
             copies[1].start()
             for n in range(2, len(copies)):
@@ -277,71 +285,65 @@
 
     def pass_on(j, e, up):
         slot = j - 1 if up else j
-        buf = ub if up else db
-        copy = hop(j, e, up, False)
+        buf = lu if up else ld
+        copy = send_sum(j, e, up, False)
         copy.wait_recv()
-        add_into(buf.at[slot, e], buf.at[slot, e], part_ref.at[e, j], width)
-        copy.start()
-
-    for home, near in ((1, True), (2, False)):
-        far, mid = (3, 2) if near else (0, 1)
-        back = 0 if near else 3
-        events = [(far, 0, near), (far, 1, near), (back, 0, not near), (mid, 0, near), (back, 1, not near), (mid, 1, near)]
-
-        @pl.when(zl == home)
+        add_into(buf.at[slot, e], buf.at[slot, e], line_ref.at[e, j], near)
+        copy.start()
+
+    for seat, up in ((1, True), (2, False)):
+        end, inner, start = (3, 2, 0) if up else (0, 1, 3)
+        events = [(end, 0, up), (end, 1, up), (start, 0, not up), (inner, 0, up), (start, 1, not up), (inner, 1, up)]
+
+        @pl.when(zl == seat)
         def _():
             for event in events:
                 pass_on(*event)
             for j, e, up in events:
-                hop(j, e, up, False).wait_send()
+                send_sum(j, e, up, False).wait_send()
     for ju, jd in order:
         for e in range(experts):
             @pl.when(zl == ju)
             def _():
-                hop(ju, e, True, False).wait_recv()
+                send_sum(ju, e, True, False).wait_recv()
 
             @pl.when(zl == jd)
             def _():
-                hop(jd, e, False, False).wait_recv()
+                send_sum(jd, e, False, False).wait_recv()
     for e in range(experts):
         @pl.when(zl == 0)
         def _():
-            add_into(out_ref.at[e], part_ref.at[e, 0], db.at[0, e], width)
+            add_into(summed.at[e], line_ref.at[e, 0], ld.at[0, e], near)
 
         @pl.when(zl == NL - 1)
         def _():
-            add_into(out_ref.at[e], part_ref.at[e, NL - 1], ub.at[NL - 2, e], width)
+            add_into(summed.at[e], line_ref.at[e, NL - 1], lu.at[NL - 2, e], near)
         for mid in range(1, NL - 1):
             @pl.when(zl == mid)
             def _():
-                add_into(out_ref.at[e], part_ref.at[e, mid], ub.at[mid - 1, e], width, db.at[mid, e])
+                add_into(summed.at[e], line_ref.at[e, mid], lu.at[mid - 1, e], near, ld.at[mid, e])
+
+    @pl.loop(0, near // CHUNK)
+    def _(i):
+        part = pl.ds(pl.multiple_of(i * CHUNK, CHUNK), CHUNK)
+        y = lax.dot_general(fit_ref[...], summed[:, :, part].reshape(fit_ref.shape[0], CHUNK), turn,
+                            preferred_element_type=F32)
+        block[:, :, part] = y.reshape(cols, y.shape[0] // cols, CHUNK).astype(BF)
+
+    blocks = xy_copies(block, home, xs, xr)
     for copy in blocks:
-        copy.wait()
-    own.wait()
-
-
-def line_sum_and_plane(parts, blocks, cid):
-    experts, _, cap, width = parts.shape
-    buf = pltpu.VMEM((NL - 1, experts, cap, width), BF)
-    return pl.pallas_call(
-        line_sum_kernel,
-        out_shape=(jax.ShapeDtypeStruct((experts, cap, width), BF), jax.ShapeDtypeStruct(blocks.shape, BF)),
-        in_specs=[VMEM, ANY], out_specs=(VMEM, ANY),
-        scratch_shapes=[buf, buf, DMA((COLS - 1,)), DMA((COLS - 1,))] + [DMA((NL - 1, experts))] * 4 + [DMA],
-        compiler_params=pltpu.CompilerParams(collective_id=cid, has_side_effects=True),
-        name="line_sum_and_plane",
-    )(parts, blocks)
-
-
-def tail_kernel(part_ref, blk_ref, mine_ref, theirs_ref, out_ref, home, away, own, got, relay, ub, db,
-                xs, xr, us, ur, ds, dr, ps, pr, ls):
-    z = my_z()
-    _, rows, width = part_ref.shape
-    near = own.shape[1]
-    wide = width // 2
-    me = lax.axis_index("x") * NY + lax.axis_index("y")
-    greet(xy_devices() + [z_of(z + 1), z_of(z - 1), z_of(z + 2), z_of(z - 2)])
-    last = NZ // 2
+        copy.start()
+    home[me] = block[me]
+    for copy in fars:
+        copy.wait_recv()
+    keep.wait()
+
+    @pl.loop(0, width // HALF)
+    def _(i):
+        part = pl.ds(pl.multiple_of(i * HALF, HALF), HALF)
+        h = got2[:, :, part].reshape(pick_ref.shape[0], HALF)
+        y = lax.dot_general(pick_ref[...], h, turn, preferred_element_type=F32)
+        part_ref[:, :, part] = y.reshape(NZ, rows, HALF).astype(BF)
 
     def spot(t, up):
         return lax.rem(z + (last - t if up else t - last) + NZ, NZ)
@@ -369,17 +371,10 @@
     for t, q, up in hops:
         if fresh_of(t, q, up):
             hop(t, q, up, True).start()
-    blocks = xy_copies(blk_ref, home, xs, xr)
-    for copy in blocks:
-        copy.start()
-    keep = pltpu.make_async_copy(blk_ref.at[me], home.at[me], ls)
-    keep.start()
     serve(0)
     serve(1)
     for copy in blocks:
         copy.wait_recv()
-    keep.wait()
-    turn = (((0,), (0,)), ((), ()))
 
     @pl.loop(0, near // CHUNK)
     def _(i):
@@ -405,24 +400,30 @@
     add_into(out_ref.at[:, pl.ds(0, near)], own, got, near)
     for t, q, up in hops:
         hop(t, q, up, fresh_of(t, q, up)).wait_send()
-    for copy in first + second + blocks:
+    for copy in first + second + blocks + fars:
         copy.wait_send()
 
 
-def tail(parts, blocks, mine, theirs, cid):
-    _, rows, width = parts.shape
-    near = blocks.shape[2]
+def back(lines, fars, mine, theirs, pick2, fit1, cid):
+    experts, _, cap, near = lines.shape
+    width = fars.shape[2]
+    rows = mine.shape[1]
+    block = (COLS, mine.shape[0] // COLS, near)
     buf = pltpu.VMEM((NZ // 2, 4, rows // 2, width // 2), BF)
+    line = pltpu.VMEM((NL - 1, experts, cap, near), BF)
+    plane = DMA((COLS - 1,))
     return pl.pallas_call(
-        tail_kernel,
+        back_kernel,
         out_shape=jax.ShapeDtypeStruct((rows, near + width), BF),
-        in_specs=[VMEM, ANY, VMEM, VMEM], out_specs=VMEM,
-        scratch_shapes=[pltpu.VMEM(blocks.shape, BF), pltpu.VMEM((rows, near), BF), pltpu.VMEM((rows, near), F32),
-                        pltpu.VMEM((rows, near), BF), pltpu.VMEM((2, rows // 2, near), BF), buf, buf,
-                        DMA((COLS - 1,)), DMA((COLS - 1,))] + [DMA((NZ // 2, 4))] * 4 + [DMA((4,)), DMA((4,)), DMA],
+        in_specs=[VMEM, ANY, VMEM, VMEM, VMEM, VMEM], out_specs=VMEM,
+        scratch_shapes=[line, line, pltpu.VMEM((experts, cap, near), BF), pltpu.VMEM(fars.shape, BF),
+                        pltpu.VMEM((NZ, rows, width), BF), pltpu.VMEM(block, BF), pltpu.VMEM(block, BF),
+                        pltpu.VMEM((rows, near), BF), pltpu.VMEM((rows, near), F32), pltpu.VMEM((rows, near), BF),
+                        pltpu.VMEM((2, rows // 2, near), BF), buf, buf, plane, plane, plane, plane]
+        + [DMA((NZ // 2, 4))] * 4 + [DMA((4,))] * 2 + [DMA((NL - 1, experts))] * 4 + [DMA],
         compiler_params=pltpu.CompilerParams(collective_id=cid, has_side_effects=True),
-        name="tail",
-    )(parts, blocks, mine, theirs)
+        name="back",
+    )(lines, fars, mine, theirs, pick2, fit1)
 
 
 def hidden_kernel(x1_ref, got_ref, fit_ref, g0_ref, g1_ref, u0_ref, u1_ref, h_ref, acc):
@@ -528,10 +529,6 @@
     )(hidden, fit2, weight, d0, d1)
 
 
-def mm(a, b, dtype=BF):
-    return jnp.dot(a, b, preferred_element_type=F32).astype(dtype)
-
-
 def body(tokens, w_gate, w_up, w_down, gates, dispatch):
     rows, width = tokens.shape
     experts = w_gate.shape[0]
@@ -576,19 +573,13 @@
 
     pick_own = lax.dynamic_index_in_dim(pick1, zh, 1, keepdims=False)
     pick_other = lax.dynamic_index_in_dim(pick1, 1 - zh, 1, keepdims=False)
-    everyone, got1 = head(tokens, pick_own, pick_other, 1)
-    rows1 = mm(fit1, got1.reshape(-1, D1)).reshape(experts, cap, D1)
-    out2 = mm(pick2, everyone.reshape(NZ * rows, width - D1))
-    lines, got2, og, ou, od = line_and_plane(
-        rows1, out2.reshape(COLS, NL * experts * SLOTS, width - D1), w_gate, w_up, w_down, 3)
+    lines, got2, og, ou, od = front(tokens, pick_own, pick_other, pick2, fit1, w_gate, w_up, w_down, 1)
     x1 = lines.reshape(experts, NL * cap, D1)
     hidden = hidden_of(x1, got2.reshape(-1, width - D1), fit2, w_gate, og, w_up, ou)
     back1, back2 = down_of(hidden, fit2, weight, w_down, od)
     back1 = back1.reshape(experts, NL, cap, D1)
-    summed, home2 = line_sum_and_plane(back1, back2.reshape(COLS, NL * experts * SLOTS, width - D1), 4)
-    give1 = mm(fit1.T, summed.reshape(experts * cap, D1))
-    sums2 = mm(pick2.T, home2.reshape(-1, width - D1)).reshape(NZ, rows, width - D1)
-    return tail(sums2, give1.reshape(COLS, experts * SLOTS, D1), pick_own, pick_other, 2)
+    back2 = back2.reshape(COLS, NL * experts * SLOTS, width - D1)
+    return back(back1, back2, pick_own, pick_other, pick2, fit1, 2)
 
 
 def solution(mesh):

time: 219 us -> 204 us (0.932)
  matrix products: 12 us -> 0 us
  Pallas kernels: 189 us -> 184 us
  local copies, waits for them, and re-layouts: 7.51 us -> 9.73 us
    dot_general x4 -> x0, matrix products: 12 us -> none  [mm(): return jnp.dot(a, b, preferred_element_type=F32).astype(dtype)]
    pallas_call x4 -> x2, Pallas kernels: 168 us -> 163 us  [the longest x1 84.4 us: front(): pl.pallas_call(front_kernel, out_shape=tuple((jax.ShapeDtypeStruct(shape,...]
    convert_element_type x0 -> x3, local copies, waits for them, and re-layouts: none -> 2.22 us  [the longest x1 1.43 us: body(): pick2 = pick2.reshape(COLS * NL * experts * SLOTS, NZ * rows).astype(BF)]
where the time goes in v4:
time: 204 us; the launch traced here: 201 us
  Pallas kernels  184 us (90%)
  local copies, waits for them, and re-layouts  9.73 us (5%)
  other arithmetic  7.57 us (4%)
    pallas_call x1, Pallas kernels, front(): pl.pallas_call(front_kernel, out_shape=tuple((jax.ShapeDtypeStruct(shape,...  84.4 us
    pallas_call x1, Pallas kernels, back(): pl.pallas_call(back_kernel, out_shape=jax.ShapeDtypeStruct((rows, near +...  78.2 us
    pallas_call x1, Pallas kernels, hidden_of(): pl.pallas_call(hidden_kernel, grid=(width // CHUNK,), out_shape=jax.Shape...  10.8 us
    pallas_call x1, Pallas kernels, down_of(): pl.pallas_call(down_kernel, grid=(width // CHUNK,), out_shape=(jax.ShapeD...  10.2 us

profile of v4, /device:TPU:64, one launch (start us, length us, event | category | flops | bytes accessed | tf_op | source)
XLA Modules:
  0.0 201.0 jit_solution(6144433640846125306)
XLA Ops:
  0.0 0.1 copy.74
  0.2 1.0 copy.76
  1.2 0.8 reshape.270.wt_ref
  2.0 1.0 copy.58
  3.0 0.2 and_select_fusion.1
  3.2 3.0 %convert_reduce_fusion = s32[4,16,2,32]{3,2,1,0:T(2,128)S(1)} fusion(s32[4,16,2,32]{3,2,1,0:T(2,128)S(1)} %and_select_fusion.1, pred[32,32]{1,0:T(8,128)(4,1)S(1)} %iota_compare_fusion), kind=kLoop, calls=%fused_computation.1 | loop fusion | flops 520192 | bytes 33792 | tf_op jit(solution)/shard_map/reduce_sum | solution.py:549
  6.2 0.3 compare_select_fusion
  6.5 1.8 compare_reduce_fusion
  8.7 0.1 and_convert_fusion.2
  8.9 0.7 copy.72.fit_ref
  9.6 0.1 constant_dynamic-slice_fusion
  9.7 0.6 copy_bitcast_fusion
  10.4 0.4 broadcast_and_fusion
  10.7 0.2 reshape.269
  10.9 1.0 and_convert_fusion.1
  11.9 1.4 reshape.266.pick_ref
  13.4 0.7 and_convert_fusion
  14.1 0.7 reshape.268
  14.8 0.8 copy.75.fit_ref
  15.7 84.4 %front.1 = (bf16[2,4,32,4096]{3,2,1,0:T(8,128)(2,1)}, bf16[16,32,3072]{2,1,0:T(8,128)(2,1)}, bf16[2,7168,128]{2,1,0:T(8,128)(2,1)}, bf16[2,7168,128]{2,1,0:T(8,128)(2,1)}, bf16[2,128,7168]{2,1,0:T(8,128)(2,1)}) custom-call(bf16[32,7168]{1,0:T(8,128)(2,1)} %tok_ref.1, bf16[128,32]{1,0:T(8,128)(2,1)} %get-tuple-element.22.mine_ref, ...), custom_call_target="tpu_custom_call" | custom-call | tf_op jit(solution)/shard_map/front/pallas_call | solution.py:222
  100.0 10.8 %hidden_units.1.h_ref = bf16[2,128,256]{2,1,0:T(8,128)(2,1)} custom-call(bf16[2,128,4096]{2,1,0:T(8,128)(2,1)} %bitcast.52, bf16[512,3072]{1,0:T(8,128)(2,1)} %bitcast.49, bf16[256,512]{1,0:T(8,128)(2,1)} %copy.75.fit_ref, bf16[2,7168,128]{2,1,0:T(8,128)(2,1)} %g0_ref.1, bf16[2,7168,128]{2,1,0:T(8,128)(2,1)} %get-tuple-element.14.g1_ref, ...), custom_call_target="tpu_custom_call" | custom-call | tf_op jit(solution)/shard_map/hidden_units/pallas_call | solution.py:463
  110.8 10.2 %down_units.1 = (bf16[2,128,4096]{2,1,0:T(8,128)(2,1)}, bf16[512,3072]{1,0:T(8,128)(2,1)}) custom-call(bf16[2,128,256]{2,1,0:T(8,128)(2,1)} %hidden_units.1.h_ref, bf16[256,512]{1,0:T(8,128)(2,1)} %copy.75.fit_ref, f32[2,128,1]{2,1,0:T(8,128)} %reshape.270.wt_ref, bf16[2,128,7168]{2,1,0:T(8,128)(2,1)} %d0_ref.1, bf16[2,128,7168]{2,1,0:T(8,128)(2,1)} %get-tuple-element.16.d1_ref), custom_call_target="tpu_custom_call" | custom-call | tf_op jit(solution)/shard_map/down_units/pallas_call | solution.py:514
  121.0 78.2 %back.1 = bf16[32,7168]{1,0:T(8,128)(2,1)} custom-call(bf16[2,4,32,4096]{3,2,1,0:T(8,128)(2,1)} %bitcast.51, bf16[16,32,3072]{2,1,0:T(8,128)(2,1)} %bitcast.50, bf16[128,32]{1,0:T(8,128)(2,1)} %get-tuple-element.22.mine_ref, bf16[128,32]{1,0:T(8,128)(2,1)} %get-tuple-element.21.theirs_ref, bf16[512,256]{1,0:T(8,128)(2,1)} %reshape.266.pick_ref, ...), custom_call_target="tpu_custom_call" | custom-call | tf_op jit(solution)/shard_map/back/pallas_call | solution.py:415
  199.2 1.8 copy.93
  (17 shorter events, 0.5 us)

commit v5 on v4

--- a/solution.py
+++ b/solution.py
@@ -529,57 +529,127 @@
     )(hidden, fit2, weight, d0, d1)
 
 
+def iota(shape, dim):
+    return lax.broadcasted_iota(jnp.int32, shape, dim)
+
+
+def ones_of(mask):
+    return jnp.where(mask, 1.0, 0.0).astype(BF)
+
+
+def over(a, n):
+    return a >> (n.bit_length() - 1)
+
+
+def rest(a, n):
+    return a & (n - 1)
+
+
+def table_kernel(seat_ref, dispatch_ref, gates_ref, mine_ref, theirs_ref, pick_ref, fit1_ref, fit2_ref, wt_ref):
+    col, zh, zl, c = seat_ref[0], seat_ref[1], seat_ref[2], seat_ref[3]
+    experts = wt_ref.shape[0]
+    total, cap = dispatch_ref.shape[1], dispatch_ref.shape[2]
+    lanes = COLS * experts
+    span = pick_ref.shape[1] // NL
+    rows = span // NH
+    turn = (((0,), (0,)), ((), ()))
+    level = (((1,), (1,)), ((), ()))
+
+    who, lane = iota((total, lanes), 0), iota((total, lanes), 1)
+    chosen = ones_of(who == over(lane, experts) * (NH * experts) + zh * experts + rest(lane, experts))
+    blocks, offsets, weights = [], [], []
+    for k in range(NL):
+        v = dispatch_ref[NC * k + c]
+        for out, part in ((blocks, over(v, span)), (offsets, rest(v, span))):
+            out.append(lax.dot_general(part.astype(F32).astype(BF), chosen, turn, preferred_element_type=F32))
+        weights.append(lax.dot_general(gates_ref[NC * k + c], chosen.astype(F32), turn,
+                                       precision=lax.Precision.HIGHEST, preferred_element_type=F32))
+    block = jnp.concatenate(blocks, axis=1)
+    offset = jnp.concatenate(offsets, axis=1)
+    weight = jnp.concatenate(weights, axis=1)
+    row = iota(block.shape, 0)
+    place = jnp.zeros(block.shape, F32)
+    for first in range(cap - 1):
+        place = place + jnp.where((block == block[first:first + 1, :]) & (row > first), 1.0, 0.0)
+
+    here = jnp.where(block == col.astype(F32), offset * SLOTS + place, -1.0)
+    width = NL * lanes
+    slots = width * SLOTS
+    wide_row = iota((span, width), 0).astype(F32)
+    slot, source = iota((slots, width), 0), iota((slots, width), 1)
+    per_k = experts * SLOTS
+    slot_lane = rest(over(slot, per_k), NL) * lanes + over(slot, NL * per_k) * experts + rest(over(slot, SLOTS), experts)
+    slot_lane = slot_lane * SLOTS + rest(slot, SLOTS) - source * SLOTS
+    near, near_source = iota((lanes * SLOTS, width), 0), iota((lanes * SLOTS, width), 1)
+    near_lane = zl * (lanes * SLOTS) + near - near_source * SLOTS
+    rowed = jnp.zeros((slots, span), F32)
+    nearby = jnp.zeros((lanes * SLOTS, span), F32)
+    for w in range(SLOTS):
+        found = jnp.zeros((span, width), F32)
+        for i in range(cap):
+            found = found + jnp.where(here[i:i + 1, :] == wide_row * SLOTS + w, 1.0, 0.0)
+        found = found.astype(BF)
+        rowed = rowed + lax.dot_general(ones_of(slot_lane == w), found, level,
+                                        preferred_element_type=F32)
+        nearby = nearby + lax.dot_general(ones_of(near_lane == w), found, level,
+                                          preferred_element_type=F32)
+    rowed, nearby = rowed.astype(BF), nearby.astype(BF)
+    r, j = iota((span, NL * span), 0), iota((span, NL * span), 1)
+    spread = jnp.dot(rowed, ones_of(r == over(j, NL * rows) * rows + rest(j, rows)), preferred_element_type=F32)
+    m, j = iota(spread.shape, 0), iota(spread.shape, 1)
+    pick_ref[...] = jnp.where(rest(over(m, per_k), NL) == rest(over(j, rows), NL), spread, 0.0).astype(BF)
+    r, o = iota((span, rows), 0), iota((span, rows), 1)
+    mine_ref[...] = jnp.dot(nearby, ones_of(r == zh * rows + o), preferred_element_type=F32).astype(BF)
+    theirs_ref[...] = jnp.dot(nearby, ones_of(r == (NH - 1 - zh) * rows + o), preferred_element_type=F32).astype(BF)
+
+    def column(a, k, e):
+        at = iota((cap, width), 1) == k * lanes + col * experts + e
+        return jnp.sum(jnp.where(at, a, 0.0), axis=1, keepdims=True)
+
+    key = block * SLOTS + place
+    m = iota((1, slots), 1)
+    m_key = (over(m, NL * per_k) * SLOTS + rest(m, SLOTS)).astype(F32)
+    n = iota((1, lanes * SLOTS), 1)
+    n_key = (over(n, per_k) * SLOTS + rest(n, SLOTS)).astype(F32)
+    for e in range(experts):
+        for k in range(NL):
+            at = (e * NL + k) * cap
+            ours = (rest(over(m, per_k), NL) == k) & (rest(over(m, SLOTS), experts) == e)
+            fit2_ref[at:at + cap, :] = ones_of(column(key, k, e) == jnp.where(ours, m_key, -1.0))
+            wt_ref[e, k * cap:(k + 1) * cap, :] = column(weight, k, e)
+        ours = rest(over(n, SLOTS), experts) == e
+        fit1_ref[e * cap:(e + 1) * cap, :] = ones_of(column(key, zl, e) == jnp.where(ours, n_key, -1.0))
+
+
+def tables(seat, dispatch, gates, rows, experts):
+    cap = dispatch.shape[2]
+    small = COLS * experts * SLOTS
+    shapes = [(small, rows), (small, rows), (NL * small, NZ * rows), (experts * cap, small),
+              (experts * NL * cap, NL * small)]
+    return pl.pallas_call(
+        table_kernel,
+        out_shape=tuple(jax.ShapeDtypeStruct(shape, BF) for shape in shapes)
+        + (jax.ShapeDtypeStruct((experts, NL * cap, 1), F32),),
+        in_specs=[pl.BlockSpec(memory_space=pltpu.SMEM), VMEM, VMEM],
+        out_specs=(VMEM,) * 6,
+        name="tables",
+    )(seat, dispatch, gates)
+
+
 def body(tokens, w_gate, w_up, w_down, gates, dispatch):
     rows, width = tokens.shape
     experts = w_gate.shape[0]
     cap = dispatch.shape[-1]
-    x, y, zh = lax.axis_index("x"), lax.axis_index("y"), lax.axis_index("zh")
-    zl, c = lax.axis_index("zl"), lax.axis_index("c")
-    col = x * NY + y
-    span = NH * rows
-
-    def of_parity(a):
-        a = a.reshape(NL, NC, COLS, NH, experts, cap)
-        a = lax.dynamic_index_in_dim(a, c, 1, keepdims=False)
-        return lax.dynamic_index_in_dim(a, zh, 2, keepdims=False)
-
-    picks = of_parity(dispatch)
-    block = picks // span
-    earlier = (block[..., :, None] == block[..., None, :]) & (jnp.arange(cap)[None, :] < jnp.arange(cap)[:, None])
-    place = jnp.sum(earlier.astype(jnp.int32), axis=-1)
-
-    here = jnp.where(block == col, (picks % span) * SLOTS + place, -1)
-    table = here[..., None, None, :] == (jnp.arange(span)[None, :] * SLOTS + jnp.arange(SLOTS)[:, None])[..., None]
-    table = jnp.any(table, axis=-1)
-    pick1 = lax.dynamic_index_in_dim(table, zl, 0, keepdims=False)
-    pick1 = pick1.reshape(COLS * experts * SLOTS, NH, rows).astype(BF)
-    pick2 = table.transpose(1, 0, 2, 3, 4).reshape(COLS, NL, experts, SLOTS, NH, 1, rows)
-    pick2 = pick2 & (jnp.arange(NL)[:, None, None, None, None, None] == jnp.arange(NL)[:, None])
-    pick2 = pick2.reshape(COLS * NL * experts * SLOTS, NZ * rows).astype(BF)
-
-    mine = lax.dynamic_index_in_dim(block * SLOTS + place, col, 1, keepdims=False)
-    mine = mine.transpose(1, 0, 2)
-    fit = mine[..., None] == jnp.arange(COLS * SLOTS)
-    fit = fit.reshape(experts, NL, cap, COLS, SLOTS)
-    fit1 = lax.dynamic_index_in_dim(fit, zl, 1, keepdims=False)
-    same_e = jnp.eye(experts, dtype=bool)
-    fit1 = fit1[:, :, :, None, :] & same_e[:, None, None, :, None]
-    fit1 = fit1.reshape(experts * cap, COLS * experts * SLOTS).astype(BF)
-    same_k = jnp.eye(NL, dtype=bool)
-    fit2 = fit[:, :, :, :, None, None, :] & same_k[None, :, None, None, :, None, None] & same_e[:, None, None, None, None, :, None]
-    fit2 = fit2.reshape(experts * NL * cap, COLS * NL * experts * SLOTS).astype(BF)
-    weight = lax.dynamic_index_in_dim(of_parity(gates), col, 1, keepdims=False)
-    weight = weight.transpose(1, 0, 2).reshape(experts, NL * cap, 1)
-
-    pick_own = lax.dynamic_index_in_dim(pick1, zh, 1, keepdims=False)
-    pick_other = lax.dynamic_index_in_dim(pick1, 1 - zh, 1, keepdims=False)
-    lines, got2, og, ou, od = front(tokens, pick_own, pick_other, pick2, fit1, w_gate, w_up, w_down, 1)
+    col = lax.axis_index("x") * NY + lax.axis_index("y")
+    seat = jnp.stack([col, lax.axis_index("zh"), lax.axis_index("zl"), lax.axis_index("c")]).astype(jnp.int32)
+    mine, theirs, pick2, fit1, fit2, weight = tables(seat, dispatch, gates, rows, experts)
+    lines, got2, og, ou, od = front(tokens, mine, theirs, pick2, fit1, w_gate, w_up, w_down, 1)
     x1 = lines.reshape(experts, NL * cap, D1)
     hidden = hidden_of(x1, got2.reshape(-1, width - D1), fit2, w_gate, og, w_up, ou)
     back1, back2 = down_of(hidden, fit2, weight, w_down, od)
     back1 = back1.reshape(experts, NL, cap, D1)
     back2 = back2.reshape(COLS, NL * experts * SLOTS, width - D1)
-    return back(back1, back2, pick_own, pick_other, pick2, fit1, 2)
+    return back(back1, back2, mine, theirs, pick2, fit1, 2)
 
 
 def solution(mesh):

time: 204 us -> 196 us (0.961)
  other arithmetic: 7.57 us -> 0.66 us
  local copies, waits for them, and re-layouts: 9.73 us -> 5.28 us
  Pallas kernels: 184 us -> 187 us
    convert_element_type x6 -> x0, local copies, waits for them, and re-layouts: 3.86 us -> none  [the longest x2 1.56 us: body(): fit2.reshape(experts * NL * cap, COLS * NL * experts * SLOTS).astype(BF)]
    pallas_call x0 -> x1, Pallas kernels: none -> 3.35 us  [tables(): pl.pallas_call(table_kernel, out_shape=tuple((jax.ShapeDtypeStruct(shape,...]
    reduce_sum x1 -> x0, other arithmetic: 2.96 us -> none  [body(): place = jnp.sum(earlier.astype(jnp.int32), axis=-1)]
where the time goes in v5:
time: 196 us; the launch traced here: 193 us
  Pallas kernels  187 us (95%)
  local copies, waits for them, and re-layouts  5.28 us (3%)
    pallas_call x1, Pallas kernels, front(): pl.pallas_call(front_kernel, out_shape=tuple((jax.ShapeDtypeStruct(shape,...  84.4 us
    pallas_call x1, Pallas kernels, back(): pl.pallas_call(back_kernel, out_shape=jax.ShapeDtypeStruct((rows, near +...  78 us
    pallas_call x1, Pallas kernels, hidden_of(): pl.pallas_call(hidden_kernel, grid=(width // CHUNK,), out_shape=jax.Shape...  10.8 us
    pallas_call x1, Pallas kernels, down_of(): pl.pallas_call(down_kernel, grid=(width // CHUNK,), out_shape=(jax.ShapeD...  10.2 us
    unnamed x3, local copies, waits for them, and re-layouts  5.28 us

profile of v5, /device:TPU:64, one launch (start us, length us, event | category | flops | bytes accessed | tf_op | source)
XLA Modules:
  0.0 192.7 jit_solution(11813593338529013127)
XLA Ops:
  0.0 0.7 pad_add_fusion.seat_ref
  0.7 1.7 copy.8.gates_ref
  2.4 1.7 copy.7.dispatch_ref
  4.1 3.4 %tables.1 = (bf16[128,32]{1,0:T(8,128)(2,1)}, bf16[128,32]{1,0:T(8,128)(2,1)}, bf16[512,256]{1,0:T(8,128)(2,1)}, bf16[64,128]{1,0:T(8,128)(2,1)}, bf16[256,512]{1,0:T(8,128)(2,1)}, /*index=5*/f32[2,128,1]{2,1,0:T(8,128)}) custom-call(s32[4]{0:T(128)} %pad_add_fusion.seat_ref, s32[8,64,32]{2,1,0:T(8,128)} %copy.7.dispatch_ref, f32[8,64,32]{2,1,0:T(8,128)} %copy.8.gates_ref), custom_call_target="tpu_custom_call" | custom-call | tf_op jit(solution)/shard_map/tables/pallas_call | solution.py:629
  7.5 84.4 %front.1 = (bf16[2,4,32,4096]{3,2,1,0:T(8,128)(2,1)}, bf16[16,32,3072]{2,1,0:T(8,128)(2,1)}, bf16[2,7168,128]{2,1,0:T(8,128)(2,1)}, bf16[2,7168,128]{2,1,0:T(8,128)(2,1)}, bf16[2,128,7168]{2,1,0:T(8,128)(2,1)}) custom-call(bf16[32,7168]{1,0:T(8,128)(2,1)} %tok_ref.1, bf16[128,32]{1,0:T(8,128)(2,1)} %get-tuple-element.18.mine_ref, ...), custom_call_target="tpu_custom_call" | custom-call | tf_op jit(solution)/shard_map/front/pallas_call | solution.py:222
  91.8 10.8 %hidden_units.1.h_ref = bf16[2,128,256]{2,1,0:T(8,128)(2,1)} custom-call(bf16[2,128,4096]{2,1,0:T(8,128)(2,1)} %bitcast.11, bf16[512,3072]{1,0:T(8,128)(2,1)} %bitcast.8, bf16[256,512]{1,0:T(8,128)(2,1)} %get-tuple-element.24.fit_ref, bf16[2,7168,128]{2,1,0:T(8,128)(2,1)} %g0_ref.1, bf16[2,7168,128]{2,1,0:T(8,128)(2,1)} %get-tuple-element.25.g1_ref, ...), custom_call_target="tpu_custom_call" | custom-call | tf_op jit(solution)/shard_map/hidden_units/pallas_call | solution.py:463
  102.6 10.2 %down_units.1 = (bf16[2,128,4096]{2,1,0:T(8,128)(2,1)}, bf16[512,3072]{1,0:T(8,128)(2,1)}) custom-call(bf16[2,128,256]{2,1,0:T(8,128)(2,1)} %hidden_units.1.h_ref, bf16[256,512]{1,0:T(8,128)(2,1)} %get-tuple-element.24.fit_ref, f32[2,128,1]{2,1,0:T(8,128)} %get-tuple-element.27.wt_ref, bf16[2,128,7168]{2,1,0:T(8,128)(2,1)} %d0_ref.1, ...), custom_call_target="tpu_custom_call" | custom-call | tf_op jit(solution)/shard_map/down_units/pallas_call | solution.py:514
  112.8 78.0 %back.1 = bf16[32,7168]{1,0:T(8,128)(2,1)} custom-call(bf16[2,4,32,4096]{3,2,1,0:T(8,128)(2,1)} %bitcast.10, bf16[16,32,3072]{2,1,0:T(8,128)(2,1)} %bitcast.9, bf16[128,32]{1,0:T(8,128)(2,1)} %get-tuple-element.18.mine_ref, bf16[128,32]{1,0:T(8,128)(2,1)} %get-tuple-element.19.theirs_ref, bf16[512,256]{1,0:T(8,128)(2,1)} %get-tuple-element.20.pick_ref, ...), custom_call_target="tpu_custom_call" | custom-call | tf_op jit(solution)/shard_map/back/pallas_call | solution.py:415
  190.9 1.8 copy.10

commit v6 on v5

--- a/solution.py
+++ b/solution.py
@@ -49,10 +49,11 @@
     return [{"x": tx, "y": ty} for tx, ty in xy_targets()]
 
 
-def xy_copies(src, dst, send, recv):
+def xy_copies(src, dst, send, recv, first=0, count=None):
     me = lax.axis_index("x") * NY + lax.axis_index("y")
+    part = pl.ds(first, src.shape[1] if count is None else count)
     return [
-        remote(src.at[tx * NY + ty], dst.at[me], send.at[d], recv.at[d], {"x": tx, "y": ty})
+        remote(src.at[tx * NY + ty, part], dst.at[me, part], send.at[d], recv.at[d], {"x": tx, "y": ty})
         for d, (tx, ty) in enumerate(xy_targets())
     ]
 
@@ -84,7 +85,7 @@
 def front_kernel(tok_ref, mine_ref, theirs_ref, pick_ref, fit_ref, wg_ref, wu_ref, wd_ref,
                  line_ref, got_ref, og_ref, ou_ref, od_ref,
                  ring, other, relay, block, home, far,
-                 xs, xr, ys, yr, us, ur, ds, dr, ps, pr, lus, lur, lds, ldr, ws, wr, ls):
+                 xs, xr, ys, yr, vs, vr, us, ur, ds, dr, ps, pr, lus, lur, lds, ldr, ws, wr, ls):
     z = my_z()
     zl = lax.axis_index("zl")
     experts = line_ref.shape[0]
@@ -153,8 +154,30 @@
     for copy in blocks:
         copy.start()
     home[me] = block[me]
-    for step in range(1, last + 1):
-        serve(step)
+    fars = []
+
+    def far_part(h, send, recv):
+        count = far.shape[1] // 2
+
+        @pl.loop(0, width // HALF)
+        def _(i):
+            part = pl.ds(pl.multiple_of(i * HALF, HALF), HALF)
+            found = []
+            for p in (2 * h, 2 * h + 1):
+                k = lax.rem(zl + p + 1, NL)
+                both = jnp.concatenate([ring[k, :, part], ring[k + NL, :, part]], axis=0)
+                y = jnp.dot(pick_ref[p], both, preferred_element_type=F32)
+                found.append(y.reshape(cols, count // 2, HALF))
+            far[:, h * count:(h + 1) * count, part] = jnp.concatenate(found, axis=1).astype(BF)
+
+        copies = xy_copies(far, got_ref, send, recv, h * count, count)
+        for copy in copies:
+            copy.start()
+        fars.extend(copies)
+
+    serve(1)
+    serve(2)
+    far_part(0, ys, yr)
     for copy in blocks:
         copy.wait_recv()
 
@@ -173,16 +196,8 @@
             def _():
                 pass_on(0, e, up).start()
 
-    @pl.loop(0, width // HALF)
-    def _(i):
-        part = pl.ds(pl.multiple_of(i * HALF, HALF), HALF)
-        every = ring[:, :, part].reshape(NZ * rows, HALF)
-        y = jnp.dot(pick_ref[...], every, preferred_element_type=F32)
-        far[:, :, part] = y.reshape(cols, y.shape[0] // cols, HALF).astype(BF)
-
-    fars = xy_copies(far, got_ref, ys, yr)
-    for copy in fars:
-        copy.start()
+    serve(3)
+    far_part(1, vs, vr)
     own = pltpu.make_async_copy(far.at[me], got_ref.at[me], ls)
     own.start()
     for i in range(NL - 1):
@@ -216,7 +231,7 @@
     experts = w_gate.shape[0]
     cap = fit1.shape[0] // experts
     block = (COLS, mine.shape[0] // COLS, D1)
-    far = (COLS, pick2.shape[0] // COLS, width)
+    far = (COLS, NL * pick2.shape[1] // COLS, width)
     shapes = [(experts, NL, cap, D1), far, w_gate.shape, w_up.shape, w_down.shape]
     plane = DMA((COLS - 1,))
     return pl.pallas_call(
@@ -225,7 +240,7 @@
         in_specs=[VMEM] * 5 + [ANY] * 3, out_specs=(VMEM, ANY, ANY, ANY, ANY),
         scratch_shapes=[pltpu.VMEM((NZ, rows, width), BF), pltpu.VMEM((rows, D1), BF),
                         pltpu.VMEM((2, rows // 2, D1), BF), pltpu.VMEM(block, BF), pltpu.VMEM(block, BF),
-                        pltpu.VMEM(far, BF), plane, plane, plane, plane]
+                        pltpu.VMEM(far, BF)] + [plane] * 6
         + [DMA((NZ // 2, 4))] * 4 + [DMA((4,))] * 2 + [DMA((NL - 1, experts))] * 4 + [DMA((3,))] * 2 + [DMA],
         compiler_params=pltpu.CompilerParams(collective_id=cid, has_side_effects=True),
         name="front",
@@ -244,7 +259,7 @@
 
 def back_kernel(line_ref, far_ref, mine_ref, theirs_ref, pick_ref, fit_ref, out_ref,
                 lu, ld, summed, got2, part_ref, block, home, away, own, got, relay, ub, db,
-                xs, xr, ys, yr, us, ur, ds, dr, ps, pr, lus, lur, lds, ldr, ls):
+                xs, xr, ys, yr, vs, vr, us, ur, ds, dr, ps, pr, lus, lur, lds, ldr, ls):
     z = my_z()
     zl = lax.axis_index("zl")
     experts = line_ref.shape[0]
@@ -265,8 +280,9 @@
         return remote(src, buf.at[slot, e], send.at[slot, e], recv.at[slot, e], z_of(z + (1 if up else -1)))
 
     order = [(NL - 1 - i, i) for i in range(NL - 1)]
-    fars = xy_copies(far_ref, got2, ys, yr)
-    for copy in fars:
+    count = got2.shape[1] // 2
+    fars = [xy_copies(far_ref, got2, ys, yr, 0, count), xy_copies(far_ref, got2, vs, vr, count, count)]
+    for copy in fars[1] + fars[0]:
         copy.start()
     keep = pltpu.make_async_copy(far_ref.at[me], got2.at[me], ls)
     keep.start()
@@ -301,50 +317,6 @@
                 pass_on(*event)
             for j, e, up in events:
                 send_sum(j, e, up, False).wait_send()
-    for ju, jd in order:
-        for e in range(experts):
-            @pl.when(zl == ju)
-            def _():
-                send_sum(ju, e, True, False).wait_recv()
-
-            @pl.when(zl == jd)
-            def _():
-                send_sum(jd, e, False, False).wait_recv()
-    for e in range(experts):
-        @pl.when(zl == 0)
-        def _():
-            add_into(summed.at[e], line_ref.at[e, 0], ld.at[0, e], near)
-
-        @pl.when(zl == NL - 1)
-        def _():
-            add_into(summed.at[e], line_ref.at[e, NL - 1], lu.at[NL - 2, e], near)
-        for mid in range(1, NL - 1):
-            @pl.when(zl == mid)
-            def _():
-                add_into(summed.at[e], line_ref.at[e, mid], lu.at[mid - 1, e], near, ld.at[mid, e])
-
-    @pl.loop(0, near // CHUNK)
-    def _(i):
-        part = pl.ds(pl.multiple_of(i * CHUNK, CHUNK), CHUNK)
-        y = lax.dot_general(fit_ref[...], summed[:, :, part].reshape(fit_ref.shape[0], CHUNK), turn,
-                            preferred_element_type=F32)
-        block[:, :, part] = y.reshape(cols, y.shape[0] // cols, CHUNK).astype(BF)
-
-    blocks = xy_copies(block, home, xs, xr)
-    for copy in blocks:
-        copy.start()
-    home[me] = block[me]
-    for copy in fars:
-        copy.wait_recv()
-    keep.wait()
-
-    @pl.loop(0, width // HALF)
-    def _(i):
-        part = pl.ds(pl.multiple_of(i * HALF, HALF), HALF)
-        h = got2[:, :, part].reshape(pick_ref.shape[0], HALF)
-        y = lax.dot_general(pick_ref[...], h, turn, preferred_element_type=F32)
-        part_ref[:, :, part] = y.reshape(NZ, rows, HALF).astype(BF)
-
     def spot(t, up):
         return lax.rem(z + (last - t if up else t - last) + NZ, NZ)
 
@@ -368,8 +340,62 @@
                     add_into(buf.at[t, q], buf.at[t, q], part_ref.at[(spot(t + 1, up),) + sub(q, rows, width)], wide)
                     hop(t + 1, q, up, False).start()
 
+    def sums_of(h):
+        for copy in fars[h]:
+            copy.wait_recv()
+
+        @pl.loop(0, width // HALF)
+        def _(i):
+            part = pl.ds(pl.multiple_of(i * HALF, HALF), HALF)
+            whole = got2[:, h * count:(h + 1) * count, part].astype(F32)
+            for p in (0, 1):
+                each = whole[:, p * (count // 2):(p + 1) * (count // 2)].reshape(pick_ref.shape[1], HALF).astype(BF)
+                y = lax.dot_general(pick_ref[2 * h + p], each, turn, preferred_element_type=F32).astype(BF)
+                k = lax.rem(zl + 2 * h + p + 1, NL)
+                part_ref[k, :, part] = y[:rows]
+                part_ref[k + NL, :, part] = y[rows:]
+
+    keep.wait()
+    sums_of(1)
     for t, q, up in hops:
-        if fresh_of(t, q, up):
+        if fresh_of(t, q, up) and (t == 0 or up):
+            hop(t, q, up, True).start()
+    for ju, jd in order:
+        for e in range(experts):
+            @pl.when(zl == ju)
+            def _():
+                send_sum(ju, e, True, False).wait_recv()
+
+            @pl.when(zl == jd)
+            def _():
+                send_sum(jd, e, False, False).wait_recv()
+    for e in range(experts):
+        @pl.when(zl == 0)
+        def _():
+            add_into(summed.at[e], line_ref.at[e, 0], ld.at[0, e], near)
+
+        @pl.when(zl == NL - 1)
+        def _():
+            add_into(summed.at[e], line_ref.at[e, NL - 1], lu.at[NL - 2, e], near)
+        for mid in range(1, NL - 1):
+            @pl.when(zl == mid)
+            def _():
+                add_into(summed.at[e], line_ref.at[e, mid], lu.at[mid - 1, e], near, ld.at[mid, e])
+
+    @pl.loop(0, near // CHUNK)
+    def _(i):
+        part = pl.ds(pl.multiple_of(i * CHUNK, CHUNK), CHUNK)
+        y = lax.dot_general(fit_ref[...], summed[:, :, part].reshape(fit_ref.shape[0], CHUNK), turn,
+                            preferred_element_type=F32)
+        block[:, :, part] = y.reshape(cols, y.shape[0] // cols, CHUNK).astype(BF)
+
+    blocks = xy_copies(block, home, xs, xr)
+    for copy in blocks:
+        copy.start()
+    home[me] = block[me]
+    sums_of(0)
+    for t, q, up in hops:
+        if fresh_of(t, q, up) and t == 1 and not up:
             hop(t, q, up, True).start()
     serve(0)
     serve(1)
@@ -400,7 +426,7 @@
     add_into(out_ref.at[:, pl.ds(0, near)], own, got, near)
     for t, q, up in hops:
         hop(t, q, up, fresh_of(t, q, up)).wait_send()
-    for copy in first + second + blocks + fars:
+    for copy in first + second + blocks + fars[0] + fars[1]:
         copy.wait_send()
 
 
@@ -419,7 +445,7 @@
         scratch_shapes=[line, line, pltpu.VMEM((experts, cap, near), BF), pltpu.VMEM(fars.shape, BF),
                         pltpu.VMEM((NZ, rows, width), BF), pltpu.VMEM(block, BF), pltpu.VMEM(block, BF),
                         pltpu.VMEM((rows, near), BF), pltpu.VMEM((rows, near), F32), pltpu.VMEM((rows, near), BF),
-                        pltpu.VMEM((2, rows // 2, near), BF), buf, buf, plane, plane, plane, plane]
+                        pltpu.VMEM((2, rows // 2, near), BF), buf, buf] + [plane] * 6
         + [DMA((NZ // 2, 4))] * 4 + [DMA((4,))] * 2 + [DMA((NL - 1, experts))] * 4 + [DMA],
         compiler_params=pltpu.CompilerParams(collective_id=cid, has_side_effects=True),
         name="back",
@@ -550,7 +576,7 @@
     experts = wt_ref.shape[0]
     total, cap = dispatch_ref.shape[1], dispatch_ref.shape[2]
     lanes = COLS * experts
-    span = pick_ref.shape[1] // NL
+    span = pick_ref.shape[2]
     rows = span // NH
     turn = (((0,), (0,)), ((), ()))
     level = (((1,), (1,)), ((), ()))
@@ -576,28 +602,21 @@
     width = NL * lanes
     slots = width * SLOTS
     wide_row = iota((span, width), 0).astype(F32)
-    slot, source = iota((slots, width), 0), iota((slots, width), 1)
     per_k = experts * SLOTS
-    slot_lane = rest(over(slot, per_k), NL) * lanes + over(slot, NL * per_k) * experts + rest(over(slot, SLOTS), experts)
-    slot_lane = slot_lane * SLOTS + rest(slot, SLOTS) - source * SLOTS
-    near, near_source = iota((lanes * SLOTS, width), 0), iota((lanes * SLOTS, width), 1)
-    near_lane = zl * (lanes * SLOTS) + near - near_source * SLOTS
-    rowed = jnp.zeros((slots, span), F32)
-    nearby = jnp.zeros((lanes * SLOTS, span), F32)
+    near, source = iota((lanes * SLOTS, width), 0), iota((lanes * SLOTS, width), 1)
+    lead = near - source * SLOTS
+    picked = [jnp.zeros((lanes * SLOTS, span), F32) for _ in range(NL)]
     for w in range(SLOTS):
         found = jnp.zeros((span, width), F32)
         for i in range(cap):
             found = found + jnp.where(here[i:i + 1, :] == wide_row * SLOTS + w, 1.0, 0.0)
         found = found.astype(BF)
-        rowed = rowed + lax.dot_general(ones_of(slot_lane == w), found, level,
-                                        preferred_element_type=F32)
-        nearby = nearby + lax.dot_general(ones_of(near_lane == w), found, level,
-                                          preferred_element_type=F32)
-    rowed, nearby = rowed.astype(BF), nearby.astype(BF)
-    r, j = iota((span, NL * span), 0), iota((span, NL * span), 1)
-    spread = jnp.dot(rowed, ones_of(r == over(j, NL * rows) * rows + rest(j, rows)), preferred_element_type=F32)
-    m, j = iota(spread.shape, 0), iota(spread.shape, 1)
-    pick_ref[...] = jnp.where(rest(over(m, per_k), NL) == rest(over(j, rows), NL), spread, 0.0).astype(BF)
+        for p in range(NL):
+            at = lead + rest(zl + p + 1, NL) * (lanes * SLOTS)
+            picked[p] = picked[p] + lax.dot_general(ones_of(at == w), found, level, preferred_element_type=F32)
+    for p in range(NL):
+        pick_ref[p] = picked[p].astype(BF)
+    nearby = picked[NL - 1].astype(BF)
     r, o = iota((span, rows), 0), iota((span, rows), 1)
     mine_ref[...] = jnp.dot(nearby, ones_of(r == zh * rows + o), preferred_element_type=F32).astype(BF)
     theirs_ref[...] = jnp.dot(nearby, ones_of(r == (NH - 1 - zh) * rows + o), preferred_element_type=F32).astype(BF)
@@ -614,7 +633,7 @@
     for e in range(experts):
         for k in range(NL):
             at = (e * NL + k) * cap
-            ours = (rest(over(m, per_k), NL) == k) & (rest(over(m, SLOTS), experts) == e)
+            ours = (rest(over(m, per_k) + zl + 1, NL) == k) & (rest(over(m, SLOTS), experts) == e)
             fit2_ref[at:at + cap, :] = ones_of(column(key, k, e) == jnp.where(ours, m_key, -1.0))
             wt_ref[e, k * cap:(k + 1) * cap, :] = column(weight, k, e)
         ours = rest(over(n, SLOTS), experts) == e
@@ -624,7 +643,7 @@
 def tables(seat, dispatch, gates, rows, experts):
     cap = dispatch.shape[2]
     small = COLS * experts * SLOTS
-    shapes = [(small, rows), (small, rows), (NL * small, NZ * rows), (experts * cap, small),
+    shapes = [(small, rows), (small, rows), (NL, small, NH * rows), (experts * cap, small),
               (experts * NL * cap, NL * small)]
     return pl.pallas_call(
         table_kernel,

time: 196 us -> 194 us (0.990)
  Pallas kernels: 187 us -> 185 us
    pallas_call x1, Pallas kernels: 84.4 us -> 80.7 us  [front(): pl.pallas_call(front_kernel, out_shape=tuple((jax.ShapeDtypeStruct(shape,...]
    pallas_call x1, Pallas kernels: 78 us -> 80 us  [back(): pl.pallas_call(back_kernel, out_shape=jax.ShapeDtypeStruct((rows, near +...]
where the time goes in v6:
time: 194 us; the launch traced here: 191 us
  Pallas kernels  185 us (95%)
  local copies, waits for them, and re-layouts  5.28 us (3%)
    pallas_call x1, Pallas kernels, front(): pl.pallas_call(front_kernel, out_shape=tuple((jax.ShapeDtypeStruct(shape,...  80.7 us
    pallas_call x1, Pallas kernels, back(): pl.pallas_call(back_kernel, out_shape=jax.ShapeDtypeStruct((rows, near +...  80 us
    pallas_call x1, Pallas kernels, hidden_of(): pl.pallas_call(hidden_kernel, grid=(width // CHUNK,), out_shape=jax.Shape...  10.8 us
    pallas_call x1, Pallas kernels, down_of(): pl.pallas_call(down_kernel, grid=(width // CHUNK,), out_shape=(jax.ShapeD...  10.2 us
    unnamed x3, local copies, waits for them, and re-layouts  5.28 us

profile of v6, /device:TPU:64, one launch (start us, length us, event | category | flops | bytes accessed | tf_op | source)
XLA Modules:
  0.0 190.7 jit_solution(12496762695493773743)
XLA Ops:
  0.0 0.7 pad_add_fusion.seat_ref
  0.7 1.7 copy.8.gates_ref
  2.4 1.7 copy.7.dispatch_ref
  4.1 3.0 %tables.1 = (bf16[128,32]{1,0:T(8,128)(2,1)}, bf16[128,32]{1,0:T(8,128)(2,1)}, bf16[4,128,64]{2,1,0:T(8,128)(2,1)}, bf16[64,128]{1,0:T(8,128)(2,1)}, bf16[256,512]{1,0:T(8,128)(2,1)}, /*index=5*/f32[2,128,1]{2,1,0:T(8,128)}) custom-call(s32[4]{0:T(128)} %pad_add_fusion.seat_ref, s32[8,64,32]{2,1,0:T(8,128)} %copy.7.dispatch_ref, f32[8,64,32]{2,1,0:T(8,128)} %copy.8.gates_ref), custom_call_target="tpu_custom_call" | custom-call | tf_op jit(solution)/shard_map/tables/pallas_call | solution.py:648
  7.1 80.7 %front.1 = (bf16[2,4,32,4096]{3,2,1,0:T(8,128)(2,1)}, bf16[16,32,3072]{2,1,0:T(8,128)(2,1)}, bf16[2,7168,128]{2,1,0:T(8,128)(2,1)}, bf16[2,7168,128]{2,1,0:T(8,128)(2,1)}, bf16[2,128,7168]{2,1,0:T(8,128)(2,1)}) custom-call(bf16[32,7168]{1,0:T(8,128)(2,1)} %tok_ref.1, bf16[128,32]{1,0:T(8,128)(2,1)} %get-tuple-element.18.mine_ref, ...), custom_call_target="tpu_custom_call" | custom-call | tf_op jit(solution)/shard_map/front/pallas_call | solution.py:237
  87.8 10.8 %hidden_units.1.h_ref = bf16[2,128,256]{2,1,0:T(8,128)(2,1)} custom-call(bf16[2,128,4096]{2,1,0:T(8,128)(2,1)} %bitcast.11, bf16[512,3072]{1,0:T(8,128)(2,1)} %bitcast.8, bf16[256,512]{1,0:T(8,128)(2,1)} %get-tuple-element.24.fit_ref, bf16[2,7168,128]{2,1,0:T(8,128)(2,1)} %g0_ref.1, bf16[2,7168,128]{2,1,0:T(8,128)(2,1)} %get-tuple-element.25.g1_ref, ...), custom_call_target="tpu_custom_call" | custom-call | tf_op jit(solution)/shard_map/hidden_units/pallas_call | solution.py:489
  98.6 10.2 %down_units.1 = (bf16[2,128,4096]{2,1,0:T(8,128)(2,1)}, bf16[512,3072]{1,0:T(8,128)(2,1)}) custom-call(bf16[2,128,256]{2,1,0:T(8,128)(2,1)} %hidden_units.1.h_ref, bf16[256,512]{1,0:T(8,128)(2,1)} %get-tuple-element.24.fit_ref, f32[2,128,1]{2,1,0:T(8,128)} %get-tuple-element.27.wt_ref, bf16[2,128,7168]{2,1,0:T(8,128)(2,1)} %d0_ref.1, ...), custom_call_target="tpu_custom_call" | custom-call | tf_op jit(solution)/shard_map/down_units/pallas_call | solution.py:540
  108.8 80.0 %back.1 = bf16[32,7168]{1,0:T(8,128)(2,1)} custom-call(bf16[2,4,32,4096]{3,2,1,0:T(8,128)(2,1)} %bitcast.10, bf16[16,32,3072]{2,1,0:T(8,128)(2,1)} %bitcast.9, bf16[128,32]{1,0:T(8,128)(2,1)} %get-tuple-element.18.mine_ref, bf16[128,32]{1,0:T(8,128)(2,1)} %get-tuple-element.19.theirs_ref, bf16[4,128,64]{2,1,0:T(8,128)(2,1)} %get-tuple-element.20.pick_ref, ...), custom_call_target="tpu_custom_call" | custom-call | tf_op jit(solution)/shard_map/back/pallas_call | solution.py:441
  188.8 1.8 copy.10

commit v7 on v6

--- a/solution.py
+++ b/solution.py
@@ -509,14 +509,13 @@
 
     @pl.when(d == 0)
     def _():
-        scale[...] = jnp.zeros(scale.shape, F32)
+        held = jnp.zeros((1, scale.shape[0]), F32)
         for e in range(experts):
             fit = fit_ref[e * rows:(e + 1) * rows, :]
             placed = lax.dot_general(fit, h_ref[e], turn, preferred_element_type=F32)
             padded[:, e * units:(e + 1) * units] = placed.astype(BF)
-            wide = jnp.broadcast_to(wt_ref[e], (rows, scale.shape[1]))
-            scale[...] += lax.dot_general(fit.astype(F32), wide, turn, precision=lax.Precision.HIGHEST,
-                                          preferred_element_type=F32)
+            held = held + jnp.sum(fit.astype(F32) * wt_ref[e], axis=0, keepdims=True)
+        scale[...] = jnp.broadcast_to(held, scale.shape[::-1]).T
 
     @pl.when(d < NEAR)
     def _():

time: 194 us -> 194 us (level)
  no operation moved by 1% of the time
where the time goes in v7:
time: 194 us; the launch traced here: 190 us
  Pallas kernels  184 us (95%)
  local copies, waits for them, and re-layouts  5.28 us (3%)
    pallas_call x1, Pallas kernels, front(): pl.pallas_call(front_kernel, out_shape=tuple((jax.ShapeDtypeStruct(shape,...  80.7 us
    pallas_call x1, Pallas kernels, back(): pl.pallas_call(back_kernel, out_shape=jax.ShapeDtypeStruct((rows, near +...  79.8 us
    pallas_call x1, Pallas kernels, hidden_of(): pl.pallas_call(hidden_kernel, grid=(width // CHUNK,), out_shape=jax.Shape...  10.8 us
    pallas_call x1, Pallas kernels, down_of(): pl.pallas_call(down_kernel, grid=(width // CHUNK,), out_shape=(jax.ShapeD...  9.78 us
    unnamed x3, local copies, waits for them, and re-layouts  5.28 us

profile of v7, /device:TPU:64, one launch (start us, length us, event | category | flops | bytes accessed | tf_op | source)
XLA Modules:
  0.0 190.1 jit_solution(17072879053962262417)
XLA Ops:
  0.0 0.7 pad_add_fusion.seat_ref
  0.7 1.7 copy.8.gates_ref
  2.4 1.7 copy.7.dispatch_ref
  4.1 3.0 %tables.1 = (bf16[128,32]{1,0:T(8,128)(2,1)}, bf16[128,32]{1,0:T(8,128)(2,1)}, bf16[4,128,64]{2,1,0:T(8,128)(2,1)}, bf16[64,128]{1,0:T(8,128)(2,1)}, bf16[256,512]{1,0:T(8,128)(2,1)}, /*index=5*/f32[2,128,1]{2,1,0:T(8,128)}) custom-call(s32[4]{0:T(128)} %pad_add_fusion.seat_ref, s32[8,64,32]{2,1,0:T(8,128)} %copy.7.dispatch_ref, f32[8,64,32]{2,1,0:T(8,128)} %copy.8.gates_ref), custom_call_target="tpu_custom_call" | custom-call | tf_op jit(solution)/shard_map/tables/pallas_call | solution.py:647
  7.1 80.7 %front.1 = (bf16[2,4,32,4096]{3,2,1,0:T(8,128)(2,1)}, bf16[16,32,3072]{2,1,0:T(8,128)(2,1)}, bf16[2,7168,128]{2,1,0:T(8,128)(2,1)}, bf16[2,7168,128]{2,1,0:T(8,128)(2,1)}, bf16[2,128,7168]{2,1,0:T(8,128)(2,1)}) custom-call(bf16[32,7168]{1,0:T(8,128)(2,1)} %tok_ref.1, bf16[128,32]{1,0:T(8,128)(2,1)} %get-tuple-element.18.mine_ref, ...), custom_call_target="tpu_custom_call" | custom-call | tf_op jit(solution)/shard_map/front/pallas_call | solution.py:237
  87.8 10.8 %hidden_units.1.h_ref = bf16[2,128,256]{2,1,0:T(8,128)(2,1)} custom-call(bf16[2,128,4096]{2,1,0:T(8,128)(2,1)} %bitcast.11, bf16[512,3072]{1,0:T(8,128)(2,1)} %bitcast.8, bf16[256,512]{1,0:T(8,128)(2,1)} %get-tuple-element.24.fit_ref, bf16[2,7168,128]{2,1,0:T(8,128)(2,1)} %g0_ref.1, bf16[2,7168,128]{2,1,0:T(8,128)(2,1)} %get-tuple-element.25.g1_ref, ...), custom_call_target="tpu_custom_call" | custom-call | tf_op jit(solution)/shard_map/hidden_units/pallas_call | solution.py:489
  98.6 9.8 %down_units.1 = (bf16[2,128,4096]{2,1,0:T(8,128)(2,1)}, bf16[512,3072]{1,0:T(8,128)(2,1)}) custom-call(bf16[2,128,256]{2,1,0:T(8,128)(2,1)} %hidden_units.1.h_ref, bf16[256,512]{1,0:T(8,128)(2,1)} %get-tuple-element.24.fit_ref, f32[2,128,1]{2,1,0:T(8,128)} %get-tuple-element.27.wt_ref, bf16[2,128,7168]{2,1,0:T(8,128)(2,1)} %d0_ref.1, ...), custom_call_target="tpu_custom_call" | custom-call | tf_op jit(solution)/shard_map/down_units/pallas_call | solution.py:539
  108.4 79.8 %back.1 = bf16[32,7168]{1,0:T(8,128)(2,1)} custom-call(bf16[2,4,32,4096]{3,2,1,0:T(8,128)(2,1)} %bitcast.10, bf16[16,32,3072]{2,1,0:T(8,128)(2,1)} %bitcast.9, bf16[128,32]{1,0:T(8,128)(2,1)} %get-tuple-element.18.mine_ref, bf16[128,32]{1,0:T(8,128)(2,1)} %get-tuple-element.19.theirs_ref, bf16[4,128,64]{2,1,0:T(8,128)(2,1)} %get-tuple-element.20.pick_ref, ...), custom_call_target="tpu_custom_call" | custom-call | tf_op jit(solution)/shard_map/back/pallas_call | solution.py:441
  188.3 1.8 copy.10
